TPU v7x, 32 devices: a whole 2x2x4 slice. The times are simulated.
32 devices in a mesh: dp: 2 (over x), seq: 4 (over z), head: 4 (over y, core).
Axes of the slice: x: 2, y: 2, z: 4, core: 2. Of those that a mesh axis runs over, the one named last changes fastest.
Arguments:
- block_input: bfloat16 [4, 1024, 1536], P('dp', 'seq', 'head'), may hold values from -6 to 6
- norm_gain: bfloat16 [1536], P('head'), may hold values from 0.25 to 1.75
- w_gate: bfloat16 [1536, 3072], P(None, 'head'), may hold values from -0.15625 to 0.15625
- w_value: bfloat16 [1536, 3072], P(None, 'head'), may hold values from -0.15625 to 0.15625
- w_select: bfloat16 [1536, 256], P(None, 'head'), may hold values from -0.15625 to 0.15625
- w_step: bfloat16 [1536, 48], P(None, 'head'), may hold values from -0.15625 to 0.15625
- conv_value: float32 [4, 3072], P(None, 'head'), may hold values from -3 to 3
- bias_value: float32 [3072], P('head'), may hold values from -3 to 3
- conv_select: float32 [4, 256], P(None, 'head'), may hold values from -3 to 3
- bias_select: float32 [256], P('head'), may hold values from -3 to 3
- step_bias: float32 [48], P('head'), as said below
- decay_log: float32 [48], P('head'), may hold values from 0 to 1.4
- skip_gain: float32 [48], P('head'), may hold values from 0.5 to 1.5
- gate_gain: float32 [3072], P('head'), may hold values from 0.25 to 1.75
- w_out: bfloat16 [3072, 1536], P('head'), may hold values from -0.109375 to 0.109375
- out_cotangent: bfloat16 [4, 1024, 1536], P('dp', 'seq', 'head'), may hold values from -6 to 6
Outputs:
- block_output: bfloat16 [4, 1024, 1536], P('dp', 'seq', 'head')
- input_grad: float32 [4, 1024, 1536], P('dp', 'seq', 'head')
- grad_norm_gain: float32 [1536], P('head')
- grad_w_gate: float32 [1536, 3072], P(None, 'head')
- grad_w_value: float32 [1536, 3072], P(None, 'head')
- grad_w_select: float32 [1536, 256], P(None, 'head')
- grad_w_step: float32 [1536, 48], P(None, 'head')
- grad_conv_value: float32 [4, 3072], P(None, 'head')
- grad_bias_value: float32 [3072], P('head')
- grad_conv_select: float32 [4, 256], P(None, 'head')
- grad_bias_select: float32 [256], P('head')
- grad_step_bias: float32 [48], P('head')
- grad_decay_log: float32 [48], P('head')
- grad_skip_gain: float32 [48], P('head')
- grad_gate_gain: float32 [3072], P('head')
- grad_w_out: float32 [3072, 1536], P('head')
Inputs may be any that keep to these rules, and one draw needn't show every extreme that they name: `step_bias`: every entry lies between -12 and -4.
All inputs are finite; a program needn't handle non-finite values.
Results may differ from a plain program's by a relative error of at most 0.012.
The roundings to bfloat16 on the way count: a program that leaves them out, or rounds other values in their place, can miss the bound.
Values may be sent and summed in bfloat16 or wider, within the bound.
A program may use at most 128 MiB of HBM per device.

v0:
```python
import jax
import jax.numpy as jnp
from jax import lax
from jax.sharding import PartitionSpec as P

GROUP = 256


EPSILON = 1e-05
HIGHEST = lax.Precision.HIGHEST


def shifted(value, axis, steps):
    count = lax.axis_size(axis)
    initial, last = (max(0, -steps), min(count, count - steps))
    return lax.ppermute(value, axis, [(source, source + steps) for source in range(initial, last)])


def carried_in(value, axis, join, neutral, backward):
    count, mine = (lax.axis_size(axis), lax.axis_index(axis))
    pieces = jax.tree.map(lambda part: lax.all_gather(part, axis), value)
    if backward:
        pieces = jax.tree.map(lambda part: part[::-1], pieces)
        mine = count - 1 - mine
    total = jax.tree.map(
        lambda part, zero: jnp.full_like(part, 0) + jnp.asarray(zero, part.dtype), value, neutral
    )

    def turn(position, total):
        longer = join(total, jax.tree.map(lambda part: part[position], pieces))
        return jax.tree.map(lambda new, old: jnp.where(position < mine, new, old), longer, total)

    return lax.fori_loop(0, count - 1, turn, total)


def silu_slope(values):
    logistic = jax.nn.sigmoid(values)
    return logistic * (1.0 + values * (1.0 - logistic))


def causal_filter(extended, weight, offset, row_count):
    filtered = offset + weight[0] * extended[:, 0:row_count].astype(jnp.float32)
    for lag_index in range(1, weight.shape[0]):
        filtered = filtered + weight[lag_index] * extended[
            :, lag_index : lag_index + row_count
        ].astype(jnp.float32)
    return filtered


def filter_back(extended, slope_grad, incoming, weight, row_count):
    rim_rows = weight.shape[0] - 1
    widened = jnp.concatenate([slope_grad, incoming], axis=1)
    grad_pre = weight[0] * widened[:, rim_rows : rim_rows + row_count]
    weight_rows = [jnp.sum(slope_grad * extended[:, 0:row_count].astype(jnp.float32), axis=(0, 1))]
    for lag_index in range(1, rim_rows + 1):
        grad_pre = (
            grad_pre
            + weight[lag_index]
            * widened[:, rim_rows - lag_index : rim_rows - lag_index + row_count]
        )
        weight_rows.append(
            jnp.sum(
                slope_grad * extended[:, lag_index : lag_index + row_count].astype(jnp.float32),
                axis=(0, 1),
            )
        )
    return (grad_pre, jnp.stack(weight_rows), jnp.sum(slope_grad, axis=(0, 1)))


def compose(first_part, second_part):
    decay_first, state_first = first_part
    decay_second, state_second = second_part
    return (decay_first * decay_second, decay_second[..., None, None] * state_first + state_second)


def block_mixing(out_block, in_block, cum_block):
    length_here = cum_block.shape[0]
    causal_mask = (jnp.arange(length_here)[:, None] >= jnp.arange(length_here)[None, :])[:, :, None]
    log_gap = cum_block[:, None, :] - cum_block[None, :, :]
    decay_mat = jnp.where(causal_mask, jnp.exp(jnp.where(causal_mask, log_gap, 0.0)), 0.0)
    intersection = lax.dot_general(
        out_block, in_block, (((1,), (1,)), ((), ())), preferred_element_type=jnp.float32
    )
    return (decay_mat, intersection[..., None] * decay_mat)


def block_forward(pieces):
    out_block, in_block, cum_block, weighted_block = pieces
    decay_mat, mixing = block_mixing(out_block, in_block, cum_block)
    return jnp.einsum("qth,thp->qhp", mixing, weighted_block, precision=HIGHEST)


def block_backward(pieces):
    out_block, in_block, cum_block, grad_block, value_block, step_block = pieces
    decay_mat, mixing = block_mixing(out_block, in_block, cum_block)
    projected_part = jnp.einsum("qth,qhp->thp", mixing, grad_block, precision=HIGHEST)
    cross_dot = jnp.einsum("qhp,thp->qth", grad_block, value_block, precision=HIGHEST)
    pair_weight = jnp.sum(decay_mat * cross_dot * step_block[None, :, :], axis=-1)
    return (projected_part, pair_weight)


def body(
    block_input,
    norm_gain,
    w_gate,
    w_value,
    w_select,
    w_step,
    conv_value,
    bias_value,
    conv_select,
    bias_select,
    step_bias,
    decay_log,
    skip_gain,
    gate_gain,
    w_out,
    out_cotangent,
):
    full_input, full_gain, full_cotangent = (
        lax.all_gather(block_input, "head", axis=2, tiled=True),
        lax.all_gather(norm_gain, "head", axis=0, tiled=True),
        lax.all_gather(out_cotangent, "head", axis=2, tiled=True),
    )
    seq_count, row_count, model_width = full_input.shape
    flat_rows = seq_count * row_count
    head_count = skip_gain.shape[0]
    inner_here = w_value.shape[1]
    head_size = inner_here // head_count
    head_devices = lax.axis_size("head")
    state_size = conv_select.shape[1] * head_devices // 2
    inner_total = inner_here * head_devices
    block_count = row_count // GROUP
    block_total = seq_count * block_count
    rim_rows = conv_value.shape[0] - 1
    block_shape = (seq_count, block_count, GROUP)
    wide_input = full_input.reshape(flat_rows, model_width).astype(jnp.float32)
    gain_wide = full_gain.astype(jnp.float32)
    inverse = lax.rsqrt(jnp.mean(wide_input * wide_input, axis=1, keepdims=True) + EPSILON)
    normed = (wide_input * inverse * gain_wide).astype(jnp.bfloat16)
    gate_pre = jnp.dot(normed, w_gate, preferred_element_type=jnp.float32).astype(jnp.bfloat16)
    value_pre = (
        jnp.dot(normed, w_value, preferred_element_type=jnp.float32)
        .astype(jnp.bfloat16)
        .reshape(seq_count, row_count, inner_here)
    )
    select_pre = (
        jnp.dot(normed, w_select, preferred_element_type=jnp.float32)
        .astype(jnp.bfloat16)
        .reshape(seq_count, row_count, -1)
    )
    step_raw = jnp.dot(normed, w_step, preferred_element_type=jnp.float32)
    value_rim, select_rim = shifted(
        (value_pre[:, row_count - rim_rows :], select_pre[:, row_count - rim_rows :]), "seq", 1
    )
    value_ext = jnp.concatenate([value_rim, value_pre], axis=1)
    select_ext = jnp.concatenate([select_rim, select_pre], axis=1)
    value_conv = causal_filter(value_ext, conv_value, bias_value, row_count)
    select_conv = causal_filter(select_ext, conv_select, bias_select, row_count)
    value_act = jax.nn.silu(value_conv).astype(jnp.bfloat16)
    select_act = jax.nn.silu(select_conv).astype(jnp.bfloat16)
    select_full = lax.all_gather(select_act, "head", axis=2, tiled=True)
    in_state = select_full[..., :state_size].reshape(block_shape + (state_size,))
    out_state = select_full[..., state_size:].reshape(block_shape + (state_size,))
    in_wide = in_state.astype(jnp.float32)
    out_wide = out_state.astype(jnp.float32)
    step_arg = step_raw + step_bias
    step_size = jax.nn.softplus(step_arg).reshape(block_shape + (head_count,))
    decay_rate = -jnp.exp(decay_log)
    cumulative = jnp.cumsum(step_size * decay_rate, axis=2)
    growth = jnp.exp(cumulative)
    totals = cumulative[:, :, -1, :]
    block_decay = jnp.exp(totals)
    value_blocks = value_act.astype(jnp.float32).reshape(block_shape + (head_count, head_size))
    weighted = value_blocks * step_size[..., None]
    out_flat = out_state.reshape(block_total, GROUP, state_size)
    in_flat = in_state.reshape(block_total, GROUP, state_size)
    cum_flat = cumulative.reshape(block_total, GROUP, head_count)
    intra_part = lax.map(
        block_forward,
        (out_flat, in_flat, cum_flat, weighted.reshape(block_total, GROUP, head_count, head_size)),
    )
    intra_part = intra_part.reshape(block_shape + (head_count, head_size))
    tail_decay = jnp.exp(totals[:, :, None, :] - cumulative)
    group_states = jnp.einsum(
        "skthp,sktn->skhpn", weighted * tail_decay[..., None], in_wide, precision=HIGHEST
    )

    def local_forward(state_now, scanned):
        group_state, factor = scanned
        return (factor[..., None, None] * state_now + group_state, state_now)

    zero_state = jnp.zeros((seq_count, head_count, head_size, state_size), jnp.float32)
    local_end, local_starts = lax.scan(
        local_forward,
        zero_state,
        (jnp.moveaxis(group_states, 1, 0), jnp.moveaxis(block_decay, 1, 0)),
    )
    device_decay = jnp.exp(jnp.sum(totals, axis=1))
    identity_pair = (jnp.ones((seq_count, head_count), jnp.float32), zero_state)
    incoming = carried_in((device_decay, local_end), "seq", compose, identity_pair, False)[1]
    decay_before = jnp.exp(jnp.cumsum(totals, axis=1) - totals)
    entering = jnp.moveaxis(local_starts, 0, 1) + decay_before[..., None, None] * incoming[:, None]
    state_end = local_end + device_decay[..., None, None] * incoming
    inter_part = (
        jnp.einsum("skqn,skhpn->skqhp", out_wide, entering, precision=HIGHEST) * growth[..., None]
    )
    state_out = intra_part + inter_part
    mixed_out = (state_out + skip_gain[:, None] * value_blocks).reshape(flat_rows, inner_here)
    gate_wide = gate_pre.astype(jnp.float32)
    gate_act = jax.nn.silu(gate_wide)
    gated_values = mixed_out * gate_act
    square_sum = lax.psum(jnp.sum(gated_values * gated_values, axis=1), "head")
    gate_scale = lax.rsqrt(square_sum / inner_total + EPSILON)[:, None]
    hidden = (gated_values * gate_scale * gate_gain).astype(jnp.bfloat16)
    branch_part = jnp.dot(hidden, w_out, preferred_element_type=jnp.float32).reshape(
        seq_count, row_count, model_width
    )
    branch_sum = lax.psum_scatter(branch_part, "head", scatter_dimension=2, tiled=True)
    block_output = (block_input.astype(jnp.float32) + branch_sum).astype(jnp.bfloat16)
    rows_dims = (((0,), (0,)), ((), ()))
    cols_dims = (((1,), (1,)), ((), ()))
    cotangent = full_cotangent.reshape(flat_rows, model_width)
    grad_w_out = lax.dot_general(hidden, cotangent, rows_dims, preferred_element_type=jnp.float32)
    d_hidden = lax.dot_general(cotangent, w_out, cols_dims, preferred_element_type=jnp.float32)
    grad_gate_gain = jnp.sum(d_hidden * gated_values * gate_scale, axis=0)
    scaled = d_hidden * gate_gain
    row_dot = lax.psum(jnp.sum(scaled * gated_values, axis=1), "head")
    d_gated = gate_scale * scaled - gated_values * gate_scale**3 * (row_dot / inner_total)[:, None]
    d_mixed = d_gated * gate_act
    gate_low = (d_gated * mixed_out * silu_slope(gate_wide)).astype(jnp.bfloat16)
    d_heads = d_mixed.reshape(block_shape + (head_count, head_size))
    grad_skip_gain = jnp.sum(d_heads * value_blocks, axis=(0, 1, 2, 4))
    scaled_heads = d_heads * growth[..., None]
    local_adjoint = jnp.einsum("skqhp,skqn->skhpn", scaled_heads, out_wide, precision=HIGHEST)

    def local_backward(adjoint_now, scanned):
        group_adjoint, factor = scanned
        return (group_adjoint + factor[..., None, None] * adjoint_now, adjoint_now)

    local_start, local_ends = lax.scan(
        local_backward,
        zero_state,
        (jnp.moveaxis(local_adjoint, 1, 0), jnp.moveaxis(block_decay, 1, 0)),
        reverse=True,
    )
    from_right = carried_in((device_decay, local_start), "seq", compose, identity_pair, True)[1]
    decay_after = jnp.exp(jnp.sum(totals, axis=1, keepdims=True) - jnp.cumsum(totals, axis=1))
    adjoint = jnp.moveaxis(local_ends, 0, 1) + decay_after[..., None, None] * from_right[:, None]
    projected_part, pair_weight = lax.map(
        block_backward,
        (
            out_flat,
            in_flat,
            cum_flat,
            d_heads.reshape(block_total, GROUP, head_count, head_size),
            value_blocks.reshape(block_total, GROUP, head_count, head_size),
            step_size.reshape(block_total, GROUP, head_count),
        ),
    )
    projected = projected_part.reshape(block_shape + (head_count, head_size))
    pair_weight = pair_weight.reshape(block_shape + (GROUP,))
    projected = (
        projected
        + jnp.einsum("sktn,skhpn->skthp", in_wide, adjoint, precision=HIGHEST)
        * tail_decay[..., None]
    )
    d_value_ssd = projected * step_size[..., None]
    step_direct = jnp.sum(value_blocks * projected, axis=-1)
    d_value = d_value_ssd + skip_gain[:, None] * d_heads
    d_in = jnp.einsum("skqt,skqn->sktn", pair_weight, out_wide, precision=HIGHEST)
    d_in = d_in + jnp.einsum(
        "skthp,skhpn->sktn",
        value_blocks * (step_size * tail_decay)[..., None],
        adjoint,
        precision=HIGHEST,
    )
    d_out = jnp.einsum("skqt,sktn->skqn", pair_weight, in_wide, precision=HIGHEST)
    d_out = d_out + jnp.einsum("skqhp,skhpn->skqn", scaled_heads, entering, precision=HIGHEST)
    log_grad = jnp.sum(d_heads * state_out, axis=-1) - jnp.sum(value_blocks * d_value_ssd, axis=-1)
    flat_log = log_grad.reshape(seq_count, row_count, head_count)
    tail_sum = jnp.flip(jnp.cumsum(jnp.flip(flat_log, 1), axis=1), 1)
    boundary = jnp.sum(from_right * state_end, axis=(2, 3))
    d_rate_log = tail_sum + boundary[:, None, :]
    step_flat = step_size.reshape(seq_count, row_count, head_count)
    grad_decay_log = jnp.sum(d_rate_log * step_flat, axis=(0, 1)) * decay_rate
    d_step = step_direct.reshape(seq_count, row_count, head_count) + d_rate_log * decay_rate
    d_step_raw = d_step.reshape(flat_rows, head_count) * jax.nn.sigmoid(step_arg)
    grad_step_bias = jnp.sum(d_step_raw, axis=0)
    select_grad = jnp.concatenate([d_in, d_out], axis=-1).reshape(
        seq_count, row_count, 2 * state_size
    )
    select_own = lax.psum_scatter(select_grad, "head", scatter_dimension=2, tiled=True)
    value_slope = d_value.reshape(seq_count, row_count, inner_here) * silu_slope(value_conv)
    select_slope = select_own * silu_slope(select_conv)
    value_next, select_next = shifted(
        (value_slope[:, :rim_rows], select_slope[:, :rim_rows]), "seq", -1
    )
    d_value_pre, grad_conv_value, grad_bias_value = filter_back(
        value_ext, value_slope, value_next, conv_value, row_count
    )
    d_select_pre, grad_conv_select, grad_bias_select = filter_back(
        select_ext, select_slope, select_next, conv_select, row_count
    )
    value_low = d_value_pre.reshape(flat_rows, inner_here).astype(jnp.bfloat16)
    select_low = d_select_pre.reshape(flat_rows, -1).astype(jnp.bfloat16)
    step_low = d_step_raw.astype(jnp.bfloat16)
    grad_w_gate = lax.dot_general(normed, gate_low, rows_dims, preferred_element_type=jnp.float32)
    grad_w_value = lax.dot_general(normed, value_low, rows_dims, preferred_element_type=jnp.float32)
    grad_w_select = lax.dot_general(
        normed, select_low, rows_dims, preferred_element_type=jnp.float32
    )
    grad_w_step = lax.dot_general(normed, step_low, rows_dims, preferred_element_type=jnp.float32)
    d_normed = lax.dot_general(gate_low, w_gate, cols_dims, preferred_element_type=jnp.float32)
    d_normed = d_normed + lax.dot_general(
        value_low, w_value, cols_dims, preferred_element_type=jnp.float32
    )
    d_normed = d_normed + lax.dot_general(
        select_low, w_select, cols_dims, preferred_element_type=jnp.float32
    )
    d_normed = d_normed + lax.dot_general(
        step_low, w_step, cols_dims, preferred_element_type=jnp.float32
    )
    slice_width = model_width // head_devices
    own_input = block_input.reshape(flat_rows, slice_width).astype(jnp.float32)
    d_normed = lax.psum(d_normed, "head")
    slice_start = lax.axis_index("head") * slice_width
    grad_norm_wide = jnp.sum(d_normed * wide_input * inverse, axis=0)
    grad_norm_gain = lax.dynamic_slice_in_dim(grad_norm_wide, slice_start, slice_width)
    norm_scaled = d_normed * gain_wide
    mean_term = jnp.mean(wide_input * norm_scaled, axis=1, keepdims=True)
    own_scaled = lax.dynamic_slice_in_dim(norm_scaled, slice_start, slice_width, axis=1)
    input_grad = (
        out_cotangent.reshape(flat_rows, slice_width).astype(jnp.float32)
        + inverse * own_scaled
        - own_input * inverse**3 * mean_term
    )
    input_grad = input_grad.reshape(seq_count, row_count, slice_width)
    all_sums = lax.psum(
        (
            grad_norm_gain,
            grad_w_gate,
            grad_w_value,
            grad_w_select,
            grad_w_step,
            grad_conv_value,
            grad_bias_value,
            grad_conv_select,
            grad_bias_select,
            grad_step_bias,
            grad_decay_log,
            grad_skip_gain,
            grad_gate_gain,
            grad_w_out,
        ),
        ("dp", "seq"),
    )
    (
        grad_norm_gain,
        grad_w_gate,
        grad_w_value,
        grad_w_select,
        grad_w_step,
        grad_conv_value,
        grad_bias_value,
        grad_conv_select,
        grad_bias_select,
        grad_step_bias,
        grad_decay_log,
        grad_skip_gain,
        grad_gate_gain,
        grad_w_out,
    ) = all_sums
    return (
        block_output,
        input_grad,
        grad_norm_gain,
        grad_w_gate,
        grad_w_value,
        grad_w_select,
        grad_w_step,
        grad_conv_value,
        grad_bias_value,
        grad_conv_select,
        grad_bias_select,
        grad_step_bias,
        grad_decay_log,
        grad_skip_gain,
        grad_gate_gain,
        grad_w_out,
    )


def solution(mesh):
    in_specs = (
        P("dp", "seq", "head"),
        P("head"),
        P(None, "head"),
        P(None, "head"),
        P(None, "head"),
        P(None, "head"),
        P(None, "head"),
        P("head"),
        P(None, "head"),
        P("head"),
        P("head"),
        P("head"),
        P("head"),
        P("head"),
        P("head", None),
        P("dp", "seq", "head"),
    )
    out_specs = (
        P("dp", "seq", "head"),
        P("dp", "seq", "head"),
        P("head"),
        P(None, "head"),
        P(None, "head"),
        P(None, "head"),
        P(None, "head"),
        P(None, "head"),
        P("head"),
        P(None, "head"),
        P("head"),
        P("head"),
        P("head"),
        P("head"),
        P("head"),
        P("head", None),
    )
    return jax.shard_map(body, mesh=mesh, in_specs=in_specs, out_specs=out_specs, check_vma=False)
```

profile of v0, /device:TPU:24, one launch (start us, length us, event | category | flops | bytes accessed | tf_op | source)
XLA Modules:
  0.0 890.4 jit_solution(5036690037722105439)
XLA Ops:
  8.7 5.2 all-gather.3
  17.4 12.8 %all-gather.9.cloned.1.call-done = bf16[2,256,1536]{2,1,0:T(8,128)(2,1)} async-done(((bf16[2,256,384]{2,1,0:T(8,128)(2,1)}), bf16[2,256,1536]{2,1,0:T(8,128)(2,1)}) %all-gather.9.cloned.1.call-update) | async-done | bytes 1572880 | tf_op jit(solution)/shard_map/all_gather | solution.py:121
  39.8 3.6 convolution_convert_fusion.1
  57.7 5.8 all_gather.28
  65.5 3.0 fusion.118
  68.5 3.0 copy.261
  78.7 13.9 %all-gather = f32[8,1,1,12]{3,2,1,0:T(1,128)S(1)} all-gather(f32[2,1,1,12]{3,2,1,0:T(1,128)} %bitcast.314), channel_id=2, replica_groups=mesh['dp'=2,'seq'=4,'head'=4] {'seq'}, dimensions={0}, use_global_device_ids=true | all-gather | bytes 480 | tf_op jit(solution)/shard_map/all_gather | solution.py:21
  95.0 11.8 %while.60 = (s32[]{:T(128)}, f32[2,256,12,64]{1,3,2,0:T(8,128)}, f32[2,256,12,64]{1,3,2,0:T(8,128)}, bf16[2,256,128]{2,1,0:T(8,128)(2,1)S(1)}, bf16[2,256,128]{2...) while((s32[]{:T(128)}, f32[2,256,12,64]{1,3,2,0:T(8,128)}, f32[2,256,12,64]{1,3,2,0:T(8,128)}, ...), condition=%wide.region_4.5_spmd, body=%wide.region_3.4_spmd.sunk | while | flops 623968256 | bytes 2418777 | solution.py:179
  95.2 5.7 fusion.230
  101.1 5.7 fusion.230
  106.8 32.7 %all-gather.13.cloned.1.call-done = f32[8,12,64,128]{3,2,1,0:T(8,128)} async-done(((f32[2,12,64,128]{3,2,1,0:T(8,128)}), f32[8,12,64,128]{3,2,1,0:T(8,128)}) %all-gather.13.cloned.1.call-update) | async-done | bytes 3145744 | tf_op jit(solution)/shard_map/all_gather | solution.py:21
  139.5 4.0 while.62
  143.5 4.3 multiply_add_fusion.2
  150.4 3.1 copy.282
  153.5 4.3 multiply_reduce_fusion.5
  157.7 7.0 psum.119
  164.8 5.4 multiply_reduce_fusion
  170.2 5.7 psum.120
  176.0 5.5 fusion.91
  181.4 3.0 copy.284
  184.5 3.0 reshape_reshape.2
  187.5 3.2 fusion.100
  191.6 2.9 copy.285
  198.3 21.9 %while.61 = (s32[]{:T(128)}, f32[2,256,12,64]{1,3,2,0:T(8,128)}, f32[2,256,256]{1,2,0:T(8,128)}, f32[2,256,12,64]{1,3,2,0:T(8,128)}, bf16[2,256,128]{2,1,0:T(8,1...) while((s32[]{:T(128)}, f32[2,256,12,64]{1,3,2,0:T(8,128)}, ...), condition=%wide.region_14.15_spmd, body=%wide.region_12.14_spmd.sunk | while | flops 1232601088 | bytes 21695716 | solution.py:250
  198.5 5.9 fusion.238
  204.4 3.9 fusion.239
  209.5 5.8 fusion.238
  215.3 3.9 fusion.239
  222.3 29.6 %all-gather.15.cloned.1.call-done = f32[8,12,64,128]{3,2,1,0:T(8,128)} async-done(((f32[2,12,64,128]{3,2,1,0:T(8,128)}), f32[8,12,64,128]{3,2,1,0:T(8,128)}) %all-gather.15.cloned.1.call-update) | async-done | bytes 3145744 | tf_op jit(solution)/shard_map/all_gather | solution.py:21
  251.9 4.0 rev.14
  255.9 5.9 while.63
  261.8 3.1 fusion.113
  266.8 4.9 fusion.165
  273.7 5.1 fusion.176
  278.9 2.7 multiply_reduce_fusion.1
  281.6 3.1 copy.290
  284.7 6.0 fusion.170
  292.4 4.3 collective-permute-start.2
  307.2 4.1 convolution_add_fusion.2
  315.1 5.4 fusion.177
  320.5 3.8 fusion.164
  325.8 3.7 convolution_bitcast_fusion
  331.9 9.9 %reduce-scatter.2.cloned.1.call-done = f32[2,256,384]{2,1,0:T(8,128)} async-done(((f32[2,256,1536]{2,1,0:T(8,128)}), f32[2,256,384]{2,1,0:T(8,128)}) %reduce-scatter.2.cloned.1.call-update) | async-done | bytes 786448 | tf_op jit(solution)/shard_map/reduce_scatter | solution.py:219
  343.8 68.9 %all-reduce.7.cloned.1.call-done = f32[512,1536]{1,0:T(8,128)} async-done(((f32[512,1536]{1,0:T(8,128)}), f32[512,1536]{1,0:T(8,128)}) %all-reduce.7.cloned.1.call-update) | async-done | bytes 3145744 | tf_op jit(solution)/shard_map/psum | solution.py:326
  412.7 4.9 fusion.66
  417.6 35.1 %all-reduce.1 = (f32[384]{0:T(512)}, f32[4,768]{1,0:T(4,128)}, f32[768]{0:T(1024)}, f32[4,64]{1,0:T(4,128)}, f32[64]{0:T(128)}, /*index=5*/f32[12]{0:T(128)}, f32[12]{0:T(128)}, f32[12]{0:T(128)}, f32[768]{0:T(1024)}) all-reduce(f32[384]{0:T(512)S(1)} %dynamic_slice.78, ...), channel_id=1, replica_groups=mesh['dp'=2,'seq'=4,'head'=4] {'dp','seq'}, use_global_device_ids=true, to_apply=%region_27.28 | all-reduce | flops 5348 | bytes 42784 | tf_op jit(solution)/shard_map/psum | solution.py:339
  455.1 416.4 %all-reduce.11.cloned.1.call-done = (f32[1536,768]{1,0:T(8,128)}, f32[1536,768]{1,0:T(8,128)}, f32[1536,64]{0,1:T(8,128)}, f32[1536,12]{0,1:T(8,128)}, f32[768,1536]{1,0:T(8,128)}) async-done(((f32[1536,768]{1,0:T(8,128)}, f32[1536,768]{1,0:T(8,128)}, f32[1536,64]{0,1:T(8,128)}, f32[1536,12]{0,1:T(8,128)}, f32[768,1536]{1,0:T(8,128)}), (f32[1536,768]{1,0:T(8,128)}, f32[1536,768]{1,0:T(8,128)}, ...) | async-done | bytes 14622736 | tf_op jit(solution)/shard_map/psum | solution.py:339
  871.5 5.2 copy.395
  (346 shorter events, 95.3 us)
Async XLA Ops:
  7.2 157.6 %copy-start = (bf16[768,1536]{1,0:T(8,128)(2,1)S(1)}, bf16[768,1536]{1,0:T(8,128)(2,1)}, u32[]{:S(2)}) copy-start(bf16[768,1536]{1,0:T(8,128)(2,1)} %param.38) | copy-start | bytes 7077892
  7.2 23.0 %all-gather.9.cloned.1.call-start = ((), (), s32[]{:S(2)}) async-start(), calls=%async_computation.1 | async-start | bytes 1966080 | tf_op jit(solution)/shard_map/all_gather | solution.py:121
  7.9 131.5 %all-gather.13.cloned.1.call-start = ((), (), s32[]{:S(2)}) async-start(), calls=%async_computation.5 | async-start | bytes 3932160 | tf_op jit(solution)/shard_map/all_gather | solution.py:21
  16.0 19.5 %copy-start.80 = (f32[12]{0:T(128)}, f32[12]{0:T(128)S(1)}, u32[]{:S(2)}) copy-start(f32[12]{0:T(128)S(1)} %exponential_negate_fusion) | copy-start | bytes 148
  39.8 5.6 copy-start.4
  39.8 5.6 copy-start.32
  43.4 22.0 %copy-start.12 = (bf16[512,768]{1,0:T(8,128)(2,1)}, bf16[512,768]{1,0:T(8,128)(2,1)S(1)}, u32[]{:S(2)}) copy-start(bf16[512,768]{1,0:T(8,128)(2,1)S(1)} %convolution_convert_fusion.1) | copy-start | bytes 2359300
  44.1 21.3 %collective-permute-start = (bf16[2,3,768]{2,1,0:T(4,128)(2,1)}, bf16[2,3,768]{2,1,0:T(4,128)(2,1)}, u32[]{:S(2)}, u32[]{:S(2)}) collective-permute-start(bf16[2,3,768]{2,1,0:T(4,128)(2,1)} %slice.138), channel_id=1, source_target_pairs={{0,4},{4,8},{8,12},{1,5},{5,9},{9,13},{2,6},{6,10},{10,14},{3,7},{... | collective-permute-start | bytes 27656 | tf_op jit(solution)/shard_map/ppermute | solution.py:16
  46.0 18.4 %copy-start.36 = (bf16[512,64]{0,1:T(8,128)(2,1)}, bf16[512,64]{0,1:T(8,128)(2,1)S(1)}, u32[]{:S(2)}) copy-start(bf16[512,64]{0,1:T(8,128)(2,1)S(1)} %convolution_convert_fusion.2) | copy-start | bytes 196612
  46.1 18.4 %copy-start.30 = (bf16[8,2,8,256]{3,2,0,1:T(8,128)(2,1)}, bf16[8,2,8,256]{3,2,0,1:T(8,128)(2,1)S(1)}, u32[]{:S(2)}) copy-start(bf16[8,2,8,256]{3,2,0,1:T(8,128)(2,1)S(1)} %copy.350) | copy-start | bytes 196612
  46.8 9.2 %collective-permute-start.1 = (bf16[2,3,64]{1,2,0:T(8,128)(2,1)}, bf16[2,3,64]{1,2,0:T(8,128)(2,1)}, u32[]{:S(2)}, u32[]{:S(2)}) collective-permute-start(bf16[2,3,64]{1,2,0:T(8,128)(2,1)} %slice.143), channel_id=1, source_target_pairs={{0,4},{4,8},{8,12},{1,5},{5,9},{9,13},{2,6},{6,10},{10,14},{3,7},{... | collective-permute-start | bytes 2312 | tf_op jit(solution)/shard_map/ppermute | solution.py:16
  76.1 88.7 %all-gather.11.cloned.1.call-start = ((), (), s32[]{:S(2)}) async-start(), calls=%async_computation.3 | async-start | bytes 1966080 | tf_op jit(solution)/shard_map/all_gather | solution.py:123
  76.8 175.1 %all-gather.15.cloned.1.call-start = ((), (), s32[]{:S(2)}) async-start(), calls=%async_computation.6 | async-start | bytes 3932160 | tf_op jit(solution)/shard_map/all_gather | solution.py:21
  77.6 17.4 %copy-start.26 = (f32[2,256,12]{1,2,0:T(8,128)S(1)}, f32[2,256,12]{1,2,0:T(8,128)}, u32[]{:S(2)}) copy-start(f32[2,256,12]{1,2,0:T(8,128)} %copy.275) | copy-start | bytes 73732
  153.5 11.4 %copy-start.73 = (f32[768]{0:T(1024)S(1)}, f32[768]{0:T(1024)}, u32[]{:S(2)}) copy-start(f32[768]{0:T(1024)} %param.37) | copy-start | bytes 9220
  157.7 18.2 %copy-start.34 = (bf16[512,768]{1,0:T(8,128)(2,1)}, bf16[512,768]{1,0:T(8,128)(2,1)S(1)}, u32[]{:S(2)}) copy-start(bf16[512,768]{1,0:T(8,128)(2,1)S(1)} %get-tuple-element.584) | copy-start | bytes 2359300
  164.8 11.2 %copy-start.66 = (f32[512]{0:T(512)}, f32[512]{0:T(512)S(1)}, u32[]{:S(2)}) copy-start(f32[512]{0:T(512)S(1)} %get-tuple-element.574) | copy-start | bytes 6148
  190.8 112.8 %all-reduce.9.cloned.1.call-start = ((), (), s32[]{:S(2)}) async-start(), calls=%async_computation.7 | async-start | bytes 1048576
  198.5 5.9 copy-start.8
  198.5 5.9 copy-start.24
  209.5 5.8 copy-start.8
  209.5 5.8 copy-start.24
  255.9 5.9 copy-start.56
  266.8 75.0 %reduce-scatter.2.cloned.1.call-start = ((), (), s32[]{:S(2)}) async-start(), calls=%async_computation.2 | async-start | bytes 3932160 | tf_op jit(solution)/shard_map/reduce_scatter | solution.py:219
  271.8 140.9 %all-reduce.7.cloned.1.call-start = ((), (), s32[]{:S(2)}) async-start(), calls=%async_computation.4 | async-start | bytes 6291456 | tf_op jit(solution)/shard_map/psum | solution.py:326
  273.6 5.2 copy-start.7
  273.6 5.2 copy-start.9
  273.7 5.2 copy-start.16
  273.7 5.2 copy-start.18
  273.7 5.2 copy-start.41
  273.7 5.2 copy-start.79
  284.7 13.9 %copy-start.76 = (f32[2,12]{1,0:T(2,128)S(1)}, f32[2,12]{1,0:T(2,128)}, u32[]{:S(2)}) copy-start(f32[2,12]{1,0:T(2,128)} %get-tuple-element.560) | copy-start | bytes 292
  290.6 9.7 %copy-start.43 = (f32[2,256,12]{1,0,2:T(2,128)S(1)}, f32[2,256,12]{1,0,2:T(2,128)}, u32[]{:S(2)}) copy-start(f32[2,256,12]{1,0,2:T(2,128)} %mul.626) | copy-start | bytes 73732
  292.4 9.6 %collective-permute-start.2 = (f32[2,3,768]{2,1,0:T(4,128)}, f32[2,3,768]{2,1,0:T(4,128)}, u32[]{:S(2)}, u32[]{:S(2)}) collective-permute-start(f32[2,3,768]{2,1,0:T(4,128)} %slice.153), channel_id=1, source_target_pairs={{4,0},{8,4},{12,8},{5,1},{9,5},{13,9},{6,2},{10,6},{14,10},{7,3},{... | collective-permute-start | bytes 55304 | tf_op jit(solution)/shard_map/ppermute | solution.py:16
  296.8 5.0 copy-start.47
  305.8 5.5 collective-permute-start.3
  314.7 5.7 copy-start.68
  314.8 5.7 copy-start.75
  314.8 556.7 %all-reduce.11.cloned.1.call-start = ((), (), s32[]{:S(2)}) async-start(), calls=%async_computation.8 | async-start | bytes 29294592 | tf_op jit(solution)/shard_map/psum | solution.py:339
  315.1 5.4 copy-start.17
  315.1 5.4 copy-start.35
  315.1 5.4 copy-start.84
  330.9 10.9 %copy-start.20 = (bf16[2,256,384]{2,1,0:T(8,128)(2,1)S(1)}, bf16[2,256,384]{2,1,0:T(8,128)(2,1)}, u32[]{:S(2)}) copy-start(bf16[2,256,384]{2,1,0:T(8,128)(2,1)} %param.24) | copy-start | bytes 1179652
  343.8 73.9 %copy-start.63 = (f32[768]{0:T(1024)S(1)}, f32[768]{0:T(1024)}, u32[]{:S(2)}) copy-start(f32[768]{0:T(1024)} %get-tuple-element.461) | copy-start | bytes 9220
  343.8 73.9 %copy-start.77 = (f32[768]{0:T(1024)S(1)}, f32[768]{0:T(1024)}, u32[]{:S(2)}) copy-start(f32[768]{0:T(1024)} %get-tuple-element.454) | copy-start | bytes 9220
  343.8 109.0 %copy-start.25 = (bf16[2,256,384]{2,1,0:T(8,128)(2,1)S(1)}, bf16[2,256,384]{2,1,0:T(8,128)(2,1)}, u32[]{:S(2)}) copy-start(bf16[2,256,384]{2,1,0:T(8,128)(2,1)} %param.39) | copy-start | bytes 1179652
  871.5 5.2 copy-start.19
  871.5 9.7 %slice-start = ((s8[4718592]{0:T(1024)(128)(4,1)}), s8[4194304]{0:T(1024)(128)(4,1)S(1)}, s32[]{:S(2)}) async-start(s8[4718592]{0:T(1024)(128)(4,1)} %bitcast.285), calls=%async_computation.9 | async-start | bytes 8388608
  (57 other events, 144.9 us)
Sparse Core Ops, SparseCore 0:
  9.6 20.5 all-gather.8
  76.2 63.2 all-gather.12
  141.0 20.8 all-gather.10
  190.9 61.0 all-gather.14
  266.9 34.7 all-reduce.8
  304.0 37.7 reduce-scatter.1
  344.2 68.4 all-reduce.6
  419.0 452.3 all-reduce.10
where the time goes:
time: 903 us; the launch traced here: 890 us
  waiting for transfers between devices  572 us (63%)
  matrix products  99 us (11%)
  blocking collectives  72.8 us (8%)
  local copies, waits for them, and re-layouts  70 us (8%)
  other arithmetic  51.2 us (6%)
  between operations  16.2 us (2%)
  starting transfers between devices  9.16 us (1%)
    psum x1, waiting for transfers between devices, body(): lax.psum((grad_norm_gain, grad_w_gate, grad_w_value, grad_w_select, grad_...  416 us
    psum x1, waiting for transfers between devices, body(): d_normed = lax.psum(d_normed, 'head')  68.9 us
    all_gather x2, waiting for transfers between devices, carried_in(): pieces = jax.tree.map(lambda part: lax.all_gather(part, axis), value)  62.4 us
    psum x1, blocking collectives, body(): lax.psum((grad_norm_gain, grad_w_gate, grad_w_value, grad_w_select, grad_...  35.1 us
    unnamed x184, local copies, waits for them, and re-layouts  23.4 us
  transfers between devices with their start and end apart: 12, of which 6 were waited for; matrix products, arithmetic and copies ran while one was open for 16% of the time, Pallas kernels for 0%

commit v1 on v0

v1 whole, which is shorter than its diff:
```python
import functools
from types import SimpleNamespace

import jax
import jax.numpy as jnp
from jax import lax
from jax.experimental import pallas as pl
from jax.experimental.pallas import tpu as pltpu
from jax.sharding import PartitionSpec as P

EPSILON = 1e-05
LOW = jnp.bfloat16
WIDE = jnp.float32
MESH = pl.DeviceIdType.MESH
RIM = 8
NEVER = -1e30
HEAD, SEQ, DP = "head", "seq", "dp"


def product(left, right, left_dim=1, right_dim=0):
    return lax.dot_general(
        left,
        right,
        (((left_dim,), (right_dim,)), ((), ())),
        preferred_element_type=WIDE,
    )


def pieces_of(values, count):
    found = []
    for _ in range(count):
        low = values.astype(LOW)
        found.append(low)
        values = values - low.astype(WIDE)
    return found


def picked(left, table, left_dim=1, table_dim=0, count=3):
    parts = [product(part, table, left_dim, table_dim) for part in pieces_of(left, count)]
    return functools.reduce(jnp.add, parts[::-1])


def picked_by(table, right, table_dim=1, right_dim=0, count=3):
    parts = [product(table, part, table_dim, right_dim) for part in pieces_of(right, count)]
    return functools.reduce(jnp.add, parts[::-1])


def iota(shape, dim):
    return lax.broadcasted_iota(jnp.int32, shape, dim)


def sigmoid(values):
    return 1.0 / (1.0 + jnp.exp(-values))


def softplus(values):
    return jnp.maximum(values, 0.0) + jnp.log1p(jnp.exp(-jnp.abs(values)))


def block(start, size):
    return pl.ds(pl.multiple_of(start, size), size)


class Links:
    def __init__(self, send_sem, recv_sem):
        self.send_sem, self.recv_sem, self.count = send_sem, recv_sem, 0

    def reserve(self, number):
        first = self.count
        self.count += number
        return first

    def copy(self, source, target, where, slot=None):
        slot = self.reserve(1) if slot is None else slot
        return pltpu.make_async_remote_copy(
            src_ref=source,
            dst_ref=target,
            send_sem=self.send_sem.at[slot],
            recv_sem=self.recv_sem.at[slot],
            device_id=where,
            device_id_type=MESH,
        )


def mixer_kernel(size, *refs):
    r = SimpleNamespace(**dict(zip(size.names, refs, strict=True)))
    seqs, rows, heads, width = size.seqs, size.rows, size.heads, size.width
    inner, state, piece = size.inner, size.state, size.piece
    head_count, seq_count, dp_count = size.head_axis, size.seq_axis, size.dp_axis
    inner_total, model = inner * head_count, piece * head_count
    total_rows = seqs * rows
    half = state // 2
    links = Links(r.send_sem, r.recv_sem)
    h, s, d = lax.axis_index(HEAD), lax.axis_index(SEQ), lax.axis_index(DP)
    side, over, across = h ^ 1, h ^ 2, h ^ 3
    place = lax.rem(h, 2) * half
    spare = half - place

    loads = []
    weights = (
        (r.w_value, r.v_w_value),
        (r.w_gate, r.v_w_gate),
        (r.w_out, r.v_w_out),
    )
    for index, (source, target) in enumerate(weights):
        load = pltpu.make_async_copy(source, target, r.load_sem.at[index])
        load.start()
        loads.append(load)

    barrier = pltpu.get_barrier_semaphore()
    peers = [{HEAD: lax.rem(h + j, head_count)} for j in range(1, head_count)]
    peers += [{SEQ: lax.rem(s + j, seq_count)} for j in range(1, seq_count)]
    peers += [{DP: lax.rem(d + j, dp_count)} for j in range(1, dp_count)]
    for peer in peers:
        pl.semaphore_signal(barrier, inc=1, device_id=peer, device_id_type=MESH)
    pl.semaphore_wait(barrier, len(peers))

    def gather_start(own, held):
        near = links.copy(own, held.at[h], {HEAD: side})
        far = links.copy(own, held.at[h], {HEAD: over})
        far.start()
        near.start()
        return (near, far)

    def gather_pass(held, pair):
        pair[1].wait_recv()
        forward = links.copy(held.at[over], held.at[over], {HEAD: side})
        forward.start()
        return pair + (forward,)

    def gather_end(copies):
        copies[0].wait_recv()
        copies[2].wait_recv()
        for copy in copies:
            copy.wait_send()

    r.gain_all[h] = jnp.broadcast_to(r.vec[0:1, size.norm_at : size.norm_at + piece], (8, piece))
    gain_copies = gather_start(r.gain_all.at[h], r.gain_all)
    input_copies = gather_start(r.x, r.x_all)
    cot_copies = gather_start(r.cot, r.cot_all)

    own_x = pltpu.make_async_copy(r.x, r.x_all.at[h], r.load_sem.at[3])
    own_cot = pltpu.make_async_copy(r.cot, r.cot_all.at[h], r.load_sem.at[4])
    own_x.start()
    own_cot.start()

    odd = lax.rem(h, 2) == 1
    r.expand[...] = jnp.where(
        (iota((state, inner), 1) // width + spare) == iota((state, inner), 0), 1.0, 0.0
    ).astype(LOW)
    lower = iota((rows, rows), 0) >= iota((rows, rows), 1)
    r.tri[...] = jnp.where(lower, 1.0, 0.0).astype(LOW)
    shift = jnp.where(iota((half, state), 0) + place == iota((half, state), 1), 1.0, 0.0).astype(LOW)
    r.taps[0:4, :] = picked(r.conv_select[...], shift)
    few = jnp.broadcast_to(r.vec[0:1, size.select_at : size.select_at + half], (8, half))
    r.taps[4:5, :] = picked(few, shift)[0:1, :]
    for row, start in enumerate((size.bias_at, size.decay_at, size.skip_at)):
        low_lanes = jnp.broadcast_to(r.vec[0:1, start : start + state], (8, state))
        r.taps[5 + row : 6 + row, :] = jnp.where(odd, low_lanes, pltpu.roll(low_lanes, half, 1))[0:1, :]
    r.v_w_select[...] = jnp.zeros((state, model), LOW)
    r.v_w_select[pl.ds(pl.multiple_of(place, half), half), :] = r.w_select[...]
    padded = jnp.concatenate([r.w_step[...], jnp.zeros((16 - heads, model), LOW)], axis=0)
    r.v_w_select[pl.ds(pl.multiple_of(spare, half), 16), :] = padded

    @pl.when(s == 0)
    def _():
        r.value_ext[:, 0:RIM, :] = jnp.zeros((seqs, RIM, inner), WIDE)
        r.select_ext[:, 0:RIM, :] = jnp.zeros((seqs, RIM, state), WIDE)
        r.state_in[...] = jnp.zeros((seqs, inner, state), LOW)

    @pl.when(s == seq_count - 1)
    def _():
        r.slope_v[:, rows : rows + RIM, :] = jnp.zeros((seqs, RIM, inner), WIDE)
        r.slope_s[:, rows : rows + RIM, :] = jnp.zeros((seqs, RIM, state), WIDE)
        r.adj_in[...] = jnp.zeros((seqs, inner, state), LOW)

    gain_copies = gather_pass(r.gain_all, gain_copies)
    input_copies = gather_pass(r.x_all, input_copies)
    gather_end(gain_copies)
    gather_end(input_copies)
    own_x.wait()

    def norm_rows(i, _):
        at = block(i * 64, 64)
        total = jnp.zeros((64, 1), WIDE)
        for k in range(head_count):
            part = r.x_all[k, at, :].astype(WIDE)
            total = total + jnp.sum(part * part, axis=1, keepdims=True)
        inverse = lax.rsqrt(total / model + EPSILON)
        r.inverse[at, :] = jnp.broadcast_to(inverse, (64, state))
        for k in range(head_count):
            part = r.x_all[k, at, :].astype(WIDE)
            r.normed[at, k * piece : (k + 1) * piece] = (
                part * inverse * r.gain_all[k, 0:1, :]
            ).astype(LOW)
        return 0

    lax.fori_loop(0, total_rows // 64, norm_rows, 0)

    for q in range(seqs):
        at = pl.ds(q * rows, rows)
        both = product(r.normed[at, :], r.v_w_select[...], 1, 1)
        r.step_arg[q] = both + r.taps[5:6, :]
        r.select_ext[q, RIM : RIM + rows, :] = both.astype(LOW).astype(WIDE)
    loads[0].wait()

    def value_matmul(q, _):
        at = block(q * rows, rows)
        r.value_ext[q, RIM : RIM + rows, :] = (
            product(r.normed[at, :], r.v_w_value[...]).astype(LOW).astype(WIDE)
        )
        return 0

    lax.fori_loop(0, seqs, value_matmul, 0)
    rims = []
    for ext in (r.select_ext, r.value_ext):
        for q in range(seqs):
            rims.append(
                links.copy(
                    ext.at[q, rows : rows + RIM, :],
                    ext.at[q, 0:RIM, :],
                    {SEQ: lax.rem(s + 1, seq_count)},
                )
            )

    @pl.when(s < seq_count - 1)
    def _():
        for copy in rims:
            copy.start()

    cot_copies = gather_pass(r.cot_all, cot_copies)

    tri = r.tri
    for q in range(seqs):
        step = softplus(r.step_arg[q])
        r.step[q] = step
        rate = -jnp.exp(r.taps[6:7, :])
        fall = step * rate
        running = picked_by(tri[...], fall)
        r.running[q] = running
        r.running_t[q] = picked(fall, tri[...], 0, 1)

        def spread(g, _):
            pick = jnp.where(iota((state, state), 0) == spare + g, 1.0, 0.0).astype(LOW)
            r.running_x[q, :, block(g * state, state)] = picked(r.running[q], pick)
            return 0

        lax.fori_loop(0, heads, spread, 0)
        r.step_x[q] = picked(step, r.expand[...], count=2)
        last = running[rows - 1 : rows, :]
        r.scale_x[q] = picked(jnp.exp(last - running), r.expand[...], count=2)
        decay = jnp.broadcast_to(jnp.exp(r.running_t[q, :, rows - 1 : rows]), (state, state))
        r.decay_row[q] = picked_by(r.expand[...], decay, 0, 0, count=2)

    @pl.when(s > 0)
    def _():
        for copy in rims:
            copy.wait_recv()

    @pl.when(s < seq_count - 1)
    def _():
        for copy in rims:
            copy.wait_send()

    lane_row = iota((1, state), 1)
    mine = (lane_row >= place) & (lane_row < place + half)

    def convolve(ext, q, base, count, taps, bias):
        wide = ext[q, pl.ds(pl.multiple_of(base, 8), count + RIM), :]
        total = bias
        for k in range(4):
            total = total + taps[k : k + 1, :] * wide[RIM - 3 + k : RIM - 3 + k + count]
        return total

    value_bias, gate_gain = r.vec[0:1, 0:inner], r.vec[0:1, inner : 2 * inner]

    for q in range(seqs):
        conv = convolve(r.select_ext, q, 0, rows, r.taps, r.taps[4:5, :])
        act = jnp.where(mine, conv * sigmoid(conv), 0.0)
        r.select_own[q] = act.astype(LOW)
    pair = links.copy(r.select_own, r.select_side, {HEAD: side})
    pair.start()

    def value_conv(i, _):
        q, base = i // (rows // 64), lax.rem(i, rows // 64) * 64
        conv = convolve(r.value_ext, q, base, 64, r.conv_value, value_bias)
        act = (conv * sigmoid(conv)).astype(LOW)
        at = block(base, 64)
        r.act[q, at, :] = act
        r.weighted[q, at, :] = (act.astype(WIDE) * r.step_x[q, at, :]).astype(LOW)
        return 0

    lax.fori_loop(0, seqs * (rows // 64), value_conv, 0)
    pair.wait()
    r.select_pair[...] = r.select_own[...] + r.select_side[...]
    swap = links.copy(r.select_pair, r.select_over, {HEAD: over})
    swap.start()
    loads[1].wait()

    def gate_matmul(q, _):
        at = block(q * rows, rows)
        r.gate[at, :] = product(r.normed[at, :], r.v_w_gate[...]).astype(LOW)
        return 0

    lax.fori_loop(0, seqs, gate_matmul, 0)
    swap.wait()
    upper = h >= 2
    first, second = r.select_pair[...], r.select_over[...]
    r.b_all[...] = jnp.where(upper, second, first)
    r.c_all[...] = jnp.where(upper, first, second)

    for q in range(seqs):
        b = r.b_all[q]
        tailed = (r.weighted[q].astype(WIDE) * r.scale_x[q]).astype(LOW)
        r.weighted_tail[q] = tailed
        r.state_local[q] = product(tailed, b, 0, 0)
        r.gram[q] = product(r.c_all[q], b, 1, 1)
        r.scale_x[q] = picked(jnp.exp(r.running[q]), r.expand[...], count=2)

    chunk_rows = inner // 3

    chunk_total = 3 * seqs

    def hop_copy(held, sent, first, c, forward):
        at = pl.ds(pl.multiple_of(lax.rem(c, 3) * chunk_rows, 16), chunk_rows)
        to = lax.rem(s + (1 if forward else seq_count - 1), seq_count)
        return at, links.copy(sent.at[c // 3, at, :], held.at[c // 3, at, :], {SEQ: to}, first + c)

    def hop(held, local, sent, first, c, forward):
        q = c // 3
        at, copy = hop_copy(held, sent, first, c, forward)

        @pl.when((s > 0) if forward else (s < seq_count - 1))
        def _():
            copy.wait_recv()

        sent[q, at, :] = (
            local[q, at, :] + r.decay_row[q, at, :] * held[q, at, :].astype(WIDE)
        ).astype(LOW)

        @pl.when((s < seq_count - 1) if forward else (s > 0))
        def _():
            copy.start()

    half_lane = iota((rows, state), 1) < width

    def decay_of(q, g):
        column = r.running_x[q, :, block(g * state, state)]
        gap = jnp.concatenate([column] * (rows // state), axis=1) - r.running_t[q, pl.ds(spare + g, 1), :]
        return jnp.exp(jnp.where(lower, gap, NEVER))

    def forward_pair(i, _):
        q, j = i // (heads // 2), lax.rem(i, heads // 2)
        at = block(j * state, state)
        values = r.weighted[q, :, at]
        zero = jnp.zeros_like(values)
        total = jnp.zeros((rows, state), WIDE)
        for part in range(2):
            mixing = (r.gram[q] * decay_of(q, 2 * j + part)).astype(LOW)
            kept = jnp.where(half_lane if part == 0 else ~half_lane, values, zero)
            total = total + product(mixing, kept)
        r.mixed[q, :, at] = total
        return 0

    pair_total = seqs * heads // 2
    forward_first = links.reserve(chunk_total)

    def forward_slot(i, _):
        @pl.when(i < pair_total)
        def _():
            forward_pair(i, 0)

        c = i - chunk_total * s

        @pl.when((c >= 0) & (c < chunk_total))
        def _():
            hop(r.state_in, r.state_local, r.state_out, forward_first, c, True)

        return 0

    lax.fori_loop(0, pair_total, forward_slot, 0)
    gather_end(cot_copies)
    own_cot.wait()
    loads[2].wait()

    def d_hidden_matmul(q, _):
        at = block(q * rows, rows)
        total = product(r.cot_all[0, at, :], r.v_w_out[:, 0:piece], 1, 1)
        for k in range(1, head_count):
            total = total + product(
                r.cot_all[k, at, :], r.v_w_out[:, k * piece : (k + 1) * piece], 1, 1
            )
        r.projected[q] = total
        return 0

    lax.fori_loop(0, seqs, d_hidden_matmul, 0)
    lax.fori_loop(pair_total, max(pair_total, chunk_total * seq_count), forward_slot, 0)

    r.skip_x[...] = picked(jnp.broadcast_to(r.taps[7:8, :], (8, state)), r.expand[...])
    for q in range(seqs):
        r.inter[q] = product(r.c_all[q], r.state_in[q], 1, 1) * r.scale_x[q]

    tile = 32
    lanes_tile = iota((tile, state), 1)

    def gate_rows(i, _):
        q, base = i // (rows // tile), lax.rem(i, rows // tile) * tile
        at, flat = block(base, tile), block(i * tile, tile)
        mixed = (
            r.mixed[q, at, :]
            + r.inter[q, at, :]
            + r.skip_x[0:1, :] * r.act[q, at, :].astype(WIDE)
        )
        r.mixed[q, at, :] = mixed
        gate = r.gate[flat, :].astype(WIDE)
        gated = mixed * (gate * sigmoid(gate))
        squares = jnp.sum(gated * gated, axis=1, keepdims=True)
        dots = jnp.sum(gated * r.projected[q, at, :] * gate_gain, axis=1, keepdims=True)
        r.sums[flat, :] = jnp.where(lanes_tile == 0, squares, jnp.where(lanes_tile == 1, dots, 0.0))
        return 0

    lax.fori_loop(0, total_rows // tile, gate_rows, 0)
    picks = jnp.where(iota((8, state), 0) == iota((8, state), 1), 1.0, 0.0).astype(LOW)

    def row_sums(own, held):
        own[...] = picked_by(picks, r.sums[...], 1, 1)
        copies = []
        for j in range(1, head_count):
            copy = links.copy(own, held.at[j - 1], {HEAD: h ^ j})
            copy.start()
            copies.append(copy)
        return copies

    def row_sums_end(own, held, copies):
        total = own[...]
        for j, copy in enumerate(copies):
            copy.wait_recv()
            total = total + held[j]
        r.sums[...] = picked(total, picks, 0, 0)
        for copy in copies:
            copy.wait_send()

    sum_copies = row_sums(r.sum_own, r.sum_held)

    @pl.when(s < seq_count - 1)
    def _():
        for c in range(chunk_total):
            hop_copy(r.state_in, r.state_out, forward_first, c, True)[1].wait_send()

    row_sums_end(r.sum_own, r.sum_held, sum_copies)

    small = r.small
    small[...] = jnp.zeros(small.shape, WIDE)

    def norm_back(i, carry):
        gain_total, skip_total = carry
        q, base = i // (rows // tile), lax.rem(i, rows // tile) * tile
        at, flat = block(base, tile), block(i * tile, tile)
        sums = r.sums[flat, :]
        scale = lax.rsqrt(sums[:, 0:1] / inner_total + EPSILON)
        mean = scale * scale * scale * (sums[:, 1:2] / inner_total)
        mixed = r.mixed[q, at, :]
        gate = r.gate[flat, :].astype(WIDE)
        logistic = sigmoid(gate)
        gate_act = gate * logistic
        gated = mixed * gate_act
        normal = gated * scale
        grad = r.projected[q, at, :]
        gain = gate_gain
        r.hidden[flat, :] = (normal * gain).astype(LOW)
        d_gated = scale * (grad * gain) - gated * mean
        d_mixed = d_gated * gate_act
        r.d_mixed_low[q, at, :] = d_mixed.astype(LOW)
        r.d_growth[q, at, :] = (d_mixed * r.scale_x[q, at, :]).astype(LOW)
        r.gate_low[flat, :] = (
            d_gated * mixed * (logistic * (1.0 + gate * (1.0 - logistic)))
        ).astype(LOW)
        gain_part = grad * normal
        skip_part = d_mixed * r.act[q, at, :].astype(WIDE)
        for k in range(tile // 8):
            gain_total = gain_total + gain_part[k * 8 : k * 8 + 8]
            skip_total = skip_total + skip_part[k * 8 : k * 8 + 8]
        return gain_total, skip_total

    blank = jnp.zeros((8, inner), WIDE)
    gain_total, skip_total = lax.fori_loop(0, total_rows // tile, norm_back, (blank, blank))
    small[5:6, 0:inner] = jnp.sum(gain_total, axis=0, keepdims=True)
    lanes = slice(inner + state, inner + 2 * state)
    skip_total = jnp.broadcast_to(jnp.sum(skip_total, axis=0, keepdims=True), (8, inner))
    small[2:3, lanes] = picked(skip_total, r.expand[...], 1, 1)[0:1, :]

    for q in range(seqs):
        r.state_local[q] = product(r.d_growth[q], r.c_all[q], 0, 0)

    ends = (s == 0) | (s == seq_count - 1)
    inside = (s > 0) & (s < seq_count - 1)

    def rows_of(me, p):
        return pl.ds(pl.multiple_of((me.chunk * dp_count + p) * me.depth, 16), me.depth)

    def stream_start(bufs, chunk):
        part, over, up, mid, out = bufs
        me = SimpleNamespace(part=part, out=out, chunk=chunk, depth=up.shape[1])
        me.over, me.up, me.mid = over.at[chunk], up.at[chunk], mid.at[chunk]
        own = part.at[rows_of(me, d), :]
        me.copies = []
        for j in range(1, dp_count):
            to = lax.rem(d + j, dp_count)
            copy = links.copy(part.at[rows_of(me, to), :], me.over.at[j - 1], {DP: to})
            copy.start()
            me.copies.append(copy)
        me.copy_up = links.copy(own, me.up, {SEQ: s ^ 1})
        me.copy_mid = links.copy(own, me.mid, {SEQ: seq_count - 1 - s})
        me.copy_down = links.copy(me.up, me.up, {SEQ: s ^ 1})
        target = out.at[rows_of(me, d), :]
        me.keep = pltpu.make_async_copy(me.up, target, r.keep_sem.at[len(keeps)])
        keeps.append(me)
        me.copies_out = [
            links.copy(me.up, target, {DP: lax.rem(d + j, dp_count)}) for j in range(1, dp_count)
        ]
        return me

    keeps = []

    def add_rows(me, target, terms):
        depth = me.depth
        step = next(t for t in (64, 48, 16) if depth % t == 0)

        def add(i, _):
            at = pl.ds(pl.multiple_of(i * step, 16), step)
            own = pl.ds(pl.multiple_of((me.chunk * dp_count + d) * depth + i * step, 16), step)
            total = me.part[own, :].astype(WIDE)
            for term in terms:
                total = total + term[at, :].astype(WIDE)
            if target is None:
                me.part[own, :] = total.astype(LOW)
            else:
                target[at, :] = total.astype(LOW)
            return 0

        lax.fori_loop(0, depth // step, add, 0)

    def stream_a(me):
        for copy in me.copies:
            copy.wait_recv()
        add_rows(me, None, [me.over.at[j] for j in range(dp_count - 1)])

        @pl.when(ends)
        def _():
            me.copy_up.start()

    def stream_b(me):
        @pl.when(inside)
        def _():
            me.copy_up.wait_recv()
            add_rows(me, None, [me.up])
            me.copy_mid.start()

    def stream_c(me):
        @pl.when(inside)
        def _():
            me.copy_mid.wait_recv()
            add_rows(me, me.up, [me.mid])
            me.copy_down.start()

        @pl.when(ends)
        def _():
            me.copy_down.wait_recv()

        me.keep.start()
        for copy in me.copies_out:
            copy.start()

    def stream_d(me):
        for copy in me.copies_out:
            copy.wait()
        for copy in me.copies:
            copy.wait_send()
        me.keep.wait()

        @pl.when(ends)
        def _():
            me.copy_up.wait_send()

        @pl.when(inside)
        def _():
            me.copy_mid.wait_send()
            me.copy_down.wait_send()

    def big_grad(part, left, right, lanes):
        for start in range(0, part.shape[0], lanes):
            columns = slice(start, start + lanes)
            part[columns, :] = product(left[:, columns], right, 0, 0).astype(LOW)

    bufs_gate = (r.part_gate, r.over_gate, r.up_gate, r.mid_gate, r.out_gate)
    bufs_out = (r.v_w_out, r.over_out, r.up_out, r.mid_out, r.out_out)
    bufs_value = (r.part_value, r.over_value, r.up_value, r.mid_value, r.out_value)
    bufs_select = (r.part_select, r.over_select, r.up_select, r.mid_select, r.out_select)
    big_grad(r.part_gate, r.normed, r.gate_low[...], piece)
    gate_streams = [stream_start(bufs_gate, c) for c in range(r.up_gate.shape[0])]

    def spread_parts(part, near):
        copies = [
            links.copy(part.at[side], near.at[0], {HEAD: side}),
            links.copy(part.at[across], near.at[1], {HEAD: side}),
        ]
        for copy in copies:
            copy.start()
        return copies

    def spread_over(part, near, sent, far, copies):
        for copy in copies:
            copy.wait_recv()

        def add(i, _):
            at = block(i * 64, 64)
            sent[at, :] = (
                part[over, at, :].astype(WIDE) + near[1, at, :].astype(WIDE)
            ).astype(LOW)
            return 0

        lax.fori_loop(0, total_rows // 64, add, 0)
        last = links.copy(sent, far, {HEAD: over})
        last.start()
        for copy in copies:
            copy.wait_send()
        return last

    for k in range(head_count):
        r.branch[k] = product(
            r.hidden[...], r.v_w_out[:, k * piece : (k + 1) * piece]
        ).astype(LOW)
    branch_copies = spread_parts(r.branch, r.branch_near)
    for k in range(head_count):
        columns = slice(k * piece, (k + 1) * piece)
        r.v_w_out[:, columns] = product(r.hidden[...], r.cot_all[k], 0, 0).astype(LOW)
    out_streams = [stream_start(bufs_out, c) for c in range(r.up_out.shape[0])]

    r.pair_weight[...] = jnp.zeros((seqs, rows, rows), WIDE)
    r.row_part[...] = jnp.zeros((seqs, rows, state), WIDE)
    r.col_part[...] = jnp.zeros((seqs, state, rows), WIDE)
    head_lane = iota((1, state), 1)

    upper_tri = iota((rows, rows), 0) <= iota((rows, rows), 1)

    def backward_pair(i, _):
        q, j = i // (heads // 2), lax.rem(i, heads // 2)
        at = block(j * state, state)
        grads, values = r.d_mixed_low[q, :, at], r.weighted[q, :, at]
        gram = r.gram[q]
        zero = jnp.zeros_like(grads)
        total = jnp.zeros((rows, state), WIDE)
        for part in range(2):
            g = 2 * j + part
            column = r.running_x[q, :, block(g * state, state)]
            gap = r.running_t[q, pl.ds(spare + g, 1), :] - jnp.concatenate(
                [column] * (rows // state), axis=1
            )
            decay = jnp.exp(jnp.where(upper_tri, gap, NEVER))
            kept = jnp.where(half_lane if part == 0 else ~half_lane, grads, zero)
            total = total + product((gram * decay).astype(LOW), kept)
            pairs = decay * product(values, kept, 1, 1)
            r.pair_weight[q] += pairs
            flows = pairs * gram
            r.row_part[q] += jnp.where(
                head_lane == spare + g, jnp.sum(flows, axis=1, keepdims=True), 0.0
            )
            r.col_part[q, pl.ds(spare + g, 1), :] = jnp.sum(flows, axis=0, keepdims=True)
        r.projected[q, :, at] = total
        return 0

    for q in range(seqs):
        r.gram[q] = product(r.b_all[q], r.c_all[q], 1, 1)
    backward_first = links.reserve(chunk_total)

    def backward_slot(i, _):
        backward_pair(i, 0)
        c = i - 2 * (seq_count - 1 - s)

        @pl.when((c >= 0) & (c < chunk_total))
        def _():
            hop(r.adj_in, r.state_local, r.adj_out, backward_first, c, False)

        return 0

    slots = chunk_total + 2 * (seq_count - 1)
    assert slots <= pair_total, slots
    lax.fori_loop(0, 5, backward_slot, 0)
    branch_last = spread_over(r.branch, r.branch_near, r.sent, r.branch_far, branch_copies)
    lax.fori_loop(5, 8, backward_slot, 0)
    stream_a(gate_streams[0])
    lax.fori_loop(8, pair_total, backward_slot, 0)

    for q in range(seqs):
        pairs = r.pair_weight[q].astype(LOW)
        d_in = product(pairs, r.c_all[q]) + product(r.weighted_tail[q], r.adj_in[q])
        d_out = product(pairs, r.b_all[q], 0, 0) + product(r.d_growth[q], r.state_in[q])
        r.sel_keep[q] = jnp.where(upper, d_out, d_in)
        r.sel_send[q] = jnp.where(upper, d_in, d_out).astype(LOW)
    sel_over = links.copy(r.sel_send, r.sel_over, {HEAD: over})
    sel_over.start()

    for q in range(seqs):
        running = r.running[q]
        tail = picked(jnp.exp(running[rows - 1 : rows, :] - running), r.expand[...], count=2)
        r.mixed[q] = product(r.b_all[q], r.adj_in[q], 1, 1) * tail

    def value_back(i, _):
        q, base = i // (rows // tile), lax.rem(i, rows // tile) * tile
        at = block(base, tile)
        inter_back = r.mixed[q, at, :]
        projected = r.projected[q, at, :] + inter_back
        step_x = r.step_x[q, at, :]
        d_mixed = r.d_mixed_low[q, at, :].astype(WIDE)
        act = r.act[q, at, :].astype(WIDE)
        d_value = projected * step_x + r.skip_x[0:1, :] * d_mixed
        conv = convolve(r.value_ext, q, base, tile, r.conv_value, value_bias)
        logistic = sigmoid(conv)
        r.slope_v[q, at, :] = d_value * (logistic * (1.0 + conv * (1.0 - logistic)))
        r.projected[q, at, :] = act * projected
        r.mixed[q, at, :] = act * step_x * inter_back
        r.inter[q, at, :] = d_mixed * r.inter[q, at, :]
        return 0

    lax.fori_loop(0, total_rows // tile, value_back, 0)
    rim_back = []
    for q in range(seqs):
        rim_back.append(
            links.copy(
                r.slope_v.at[q, 0:RIM, :],
                r.slope_v.at[q, rows : rows + RIM, :],
                {SEQ: lax.rem(s + seq_count - 1, seq_count)},
            )
        )

    @pl.when(s > 0)
    def _():
        for copy in rim_back:
            copy.start()

    sel_over.wait()
    r.sel_pair[...] = (r.sel_keep[...] + r.sel_over[...].astype(WIDE)).astype(LOW)
    sel_side = links.copy(r.sel_pair, r.sel_side, {HEAD: side})
    sel_side.start()


    sel_side.wait()
    for q in range(seqs):
        total = r.sel_pair[q].astype(WIDE) + r.sel_side[q].astype(WIDE)
        conv = convolve(r.select_ext, q, 0, rows, r.taps, r.taps[4:5, :])
        logistic = sigmoid(conv)
        r.slope_s[q, 0:rows, :] = jnp.where(
            mine, total * (logistic * (1.0 + conv * (1.0 - logistic))), 0.0
        )
    rim_back_s = []
    for q in range(seqs):
        rim_back_s.append(
            links.copy(
                r.slope_s.at[q, 0:RIM, :],
                r.slope_s.at[q, rows : rows + RIM, :],
                {SEQ: lax.rem(s + seq_count - 1, seq_count)},
            )
        )

    @pl.when(s > 0)
    def _():
        for copy in rim_back_s:
            copy.start()

    @pl.when(s < seq_count - 1)
    def _():
        for copy in rim_back:
            copy.wait_recv()

    def conv_back(i, carry):
        q, base = i // (rows // tile), lax.rem(i, rows // tile) * tile
        at = block(base, tile)
        slopes = r.slope_v[q, pl.ds(pl.multiple_of(base, 8), tile + RIM), :]
        wide = r.value_ext[q, pl.ds(pl.multiple_of(base, 8), tile + RIM), :]
        grad = r.conv_value[0:1, :] * slopes[3 : 3 + tile]
        for k in range(1, 4):
            grad = grad + r.conv_value[k : k + 1, :] * slopes[3 - k : 3 - k + tile]
        r.gate[block(i * tile, tile), :] = grad.astype(LOW)
        own = slopes[0:tile]
        fresh = []
        for k in range(4):
            term = own * wide[RIM - 3 + k : RIM - 3 + k + tile]
            total = carry[k]
            for t in range(tile // 8):
                total = total + term[t * 8 : t * 8 + 8]
            fresh.append(total)
        total = carry[4]
        for t in range(tile // 8):
            total = total + own[t * 8 : t * 8 + 8]
        return tuple(fresh) + (total,)

    totals = lax.fori_loop(0, total_rows // tile, conv_back, (blank,) * 5)
    for k in range(5):
        small[k : k + 1, 0:inner] = jnp.sum(totals[k], axis=0, keepdims=True)
    big_grad(r.part_value, r.normed, r.gate[...], piece)
    value_streams = [stream_start(bufs_value, c) for c in range(r.up_value.shape[0])]
    stream_a(gate_streams[1])
    stream_b(gate_streams[0])

    for q in range(seqs):
        step = r.step[q]
        rate = -jnp.exp(r.taps[6:7, :])
        expand = r.expand[...]
        direct = picked(r.projected[q], expand, 1, 1, 2)
        later = picked(r.inter[q], expand, 1, 1, 2)
        earlier = picked(r.mixed[q], expand, 1, 1, 2)
        crossing = r.state_in[q].astype(WIDE) * r.adj_in[q].astype(WIDE)
        bound = picked(picked_by(jnp.ones((8, state), LOW), crossing, 1, 1), expand, 1, 1)[0:1, :]
        last = r.running[q, rows - 1 : rows, :]
        d_log = (
            picked_by(tri[...], later - r.row_part[q], 0, 0)
            + picked_by(tri[...], r.col_part[q], 0, 1)
            + (picked_by(tri[...], earlier) - earlier)
            + bound * jnp.exp(last)
        )
        used = (head_lane >= spare) & (head_lane < spare + heads)
        d_step = direct + d_log * rate
        d_raw = jnp.where(used, d_step * sigmoid(r.step_arg[q]), 0.0)
        r.step_grad[q] = d_raw
        lanes = slice(inner + state, inner + 2 * state)
        small[0:1, lanes] += jnp.sum(d_raw, axis=0, keepdims=True)
        small[1:2, lanes] += jnp.where(used, jnp.sum(d_log * step, axis=0, keepdims=True) * rate, 0.0)


    @pl.when(s < seq_count - 1)
    def _():
        for copy in rim_back_s:
            copy.wait_recv()

    for q in range(seqs):
        slopes = r.slope_s[q]
        wide = r.select_ext[q]
        at = slice(inner, inner + state)
        grad = r.taps[0:1, :] * slopes[3 : 3 + rows]
        for k in range(1, 4):
            grad = grad + r.taps[k : k + 1, :] * slopes[3 - k : 3 - k + rows]
        own = slopes[0:rows]
        for k in range(4):
            small[k : k + 1, at] += jnp.sum(
                own * wide[RIM - 3 + k : RIM - 3 + k + rows], axis=0, keepdims=True
            )
        small[4:5, at] += jnp.sum(own, axis=0, keepdims=True)
        r.select_low[pl.ds(q * rows, rows), :] = jnp.where(mine, grad, r.step_grad[q]).astype(LOW)
    big_grad(r.part_select, r.select_low, r.normed[...], state)
    select_stream = stream_start(bufs_select, 0)
    stream_a(out_streams[0])
    stream_b(gate_streams[1])
    stream_c(gate_streams[0])

    branch_last.wait()

    def output_rows(i, _):
        at = block(i * 64, 64)
        total = (
            r.branch[h, at, :].astype(WIDE)
            + r.branch_near[0, at, :].astype(WIDE)
            + r.branch_far[at, :].astype(WIDE)
        )
        r.o_block[at, :] = (r.x_all[h, at, :].astype(WIDE) + total).astype(LOW)
        return 0

    lax.fori_loop(0, total_rows // 64, output_rows, 0)
    for k in range(head_count):
        columns = slice(k * piece, (k + 1) * piece)

        def d_normed_rows(q, _):
            at = block(q * rows, rows)
            total = product(r.gate_low[at, :], r.v_w_gate[columns, :], 1, 1)
            total = total + product(r.gate[at, :], r.v_w_value[columns, :], 1, 1)
            total = total + product(r.select_low[at, :], r.v_w_select[:, columns])
            mean = jnp.sum(
                total * r.x_all[k, at, :].astype(WIDE) * r.gain_all[k, 0:1, :],
                axis=1,
                keepdims=True,
            )
            r.branch[k, at, :] = total.astype(LOW)
            if k == 0:
                r.sums[at, :] = jnp.where(iota((rows, state), 1) == 0, mean, 0.0)
            else:
                r.sums[at, :] += jnp.where(iota((rows, state), 1) == 0, mean, 0.0)
            return 0

        lax.fori_loop(0, seqs, d_normed_rows, 0)
    normed_copies = spread_parts(r.branch, r.normed_near)
    mean_copies = row_sums(r.mean_own, r.mean_held)
    stream_a(out_streams[1])
    stream_b(out_streams[0])
    stream_c(gate_streams[1])
    normed_last = spread_over(r.branch, r.normed_near, r.sent, r.normed_far, normed_copies)
    row_sums_end(r.mean_own, r.mean_held, mean_copies)
    normed_last.wait()

    def input_rows(i, total):
        at = block(i * 32, 32)
        grad = (
            r.branch[h, at, :].astype(WIDE)
            + r.normed_near[0, at, :].astype(WIDE)
            + r.normed_far[at, :].astype(WIDE)
        )
        own = r.x_all[h, at, :].astype(WIDE)
        inverse = r.inverse[at, 0:1]
        mean = r.sums[at, 0:1] / model
        r.o_input[at, :] = (
            r.cot_all[h, at, :].astype(WIDE)
            + inverse * (grad * r.gain_all[h, 0:1, :])
            - own * (inverse * inverse * inverse * mean)
        )
        term = grad * own * inverse
        for t in range(4):
            total = total + term[t * 8 : t * 8 + 8]
        return total

    gain_grad = lax.fori_loop(0, total_rows // 32, input_rows, jnp.zeros((8, piece), WIDE))
    small[7:8, 0:piece] = jnp.sum(gain_grad, axis=0, keepdims=True)

    small_copies = []
    for j in range(1, seq_count):
        copy = links.copy(small, r.small_seq.at[j - 1], {SEQ: lax.rem(s + j, seq_count)})
        copy.start()
        small_copies.append(copy)
    stream_a(value_streams[0])
    stream_b(out_streams[1])
    stream_c(out_streams[0])
    stream_a(value_streams[1])
    stream_b(value_streams[0])
    stream_c(out_streams[1])
    stream_a(select_stream)
    stream_b(value_streams[1])
    stream_b(select_stream)
    stream_c(value_streams[0])
    stream_c(value_streams[1])
    stream_c(select_stream)
    total = small[...]
    for j, copy in enumerate(small_copies):
        copy.wait()
    for j in range(seq_count - 1):
        total = total + r.small_seq[j]
    r.small_mid[...] = total
    small_copies = []
    for j in range(1, dp_count):
        copy = links.copy(r.small_mid, r.small_dp.at[j - 1], {DP: lax.rem(d + j, dp_count)})
        copy.start()
        small_copies.append(copy)
    for copy in small_copies:
        copy.wait()
    for j in range(dp_count - 1):
        total = total + r.small_dp[j]
    r.o_small[:, 0:inner] = total[:, 0:inner]
    taps_grad, by_head = total[:, inner : inner + state], total[:, inner + state :]
    r.o_small[:, inner : inner + state] = jnp.where(odd, pltpu.roll(taps_grad, half, 1), taps_grad)
    r.o_small[:, inner + state :] = jnp.where(odd, by_head, pltpu.roll(by_head, half, 1))
    for me in keeps:
        stream_d(me)

    @pl.when(s > 0)
    def _():
        for copy in rim_back + rim_back_s:
            copy.wait_send()
        for c in range(chunk_total):
            hop_copy(r.adj_in, r.adj_out, backward_first, c, False)[1].wait_send()

    assert links.count <= size.links, links.count


def finish_kernel(half, heads, piece, inner, *refs):
    ins, outs = refs[:7], refs[7:]
    for source, target in zip(ins[:5], outs[:5]):
        target[...] = source[...].astype(target.dtype)
    matrix, small = ins[5:]
    g_select, g_step, g_norm, g_conv, g_bias, g_conv_s, g_bias_s, g_bias_h, g_decay, g_skip, g_gain = outs[5:]

    @pl.when(pl.program_id(0) == 0)
    def _():
        odd = lax.rem(lax.axis_index(HEAD), 2) == 1
        low_rows, high_rows = matrix[0:half, :].astype(WIDE), matrix[half : 2 * half, :].astype(WIDE)
        g_select[...] = jnp.where(odd, high_rows, low_rows)
        g_step[...] = jnp.where(odd, low_rows, high_rows)[0:heads, :]
        g_norm[...] = small[7:8, 0:piece]
        g_conv[...] = small[0:4, 0:inner]
        g_bias[...] = small[4:5, 0:inner]
        g_gain[...] = small[5:6, 0:inner]
        g_conv_s[...] = small[0:4, inner : inner + half]
        g_bias_s[...] = small[4:5, inner : inner + half]
        for row, target in enumerate((g_bias_h, g_decay, g_skip)):
            target[...] = small[row : row + 1, inner + 2 * half : inner + 2 * half + heads]


def body(size, *args):
    (
        block_input,
        norm_gain,
        w_gate,
        w_value,
        w_select,
        w_step,
        conv_value,
        bias_value,
        conv_select,
        bias_select,
        step_bias,
        decay_log,
        skip_gain,
        gate_gain,
        w_out,
        out_cotangent,
    ) = args
    seqs, rows, piece = block_input.shape
    heads, inner = skip_gain.shape[0], w_value.shape[1]
    head_axis, seq_axis, dp_axis = size[HEAD], size[SEQ], size[DP]
    half = w_select.shape[1]
    state = half * head_axis // 2
    width = inner // heads
    model = piece * head_axis
    total_rows = seqs * rows
    assert head_axis == 4 and seq_axis == 4 and 2 * half == state and heads <= half and 2 * width == state

    def aligned(values):
        values = values.astype(WIDE)
        return jnp.pad(values, (0, -values.shape[0] % state))

    singles = (bias_value, gate_gain, norm_gain, bias_select, step_bias, decay_log, skip_gain)
    singles = [aligned(values) for values in singles]
    starts = [0]
    for values in singles:
        starts.append(starts[-1] + values.shape[0])
    vec = jnp.concatenate(singles)[None]
    vmem = pl.BlockSpec(memory_space=pltpu.VMEM)
    anywhere = pl.BlockSpec(memory_space=pl.ANY)
    inputs = dict(
        x=(block_input.reshape(total_rows, piece), anywhere),
        cot=(out_cotangent.reshape(total_rows, piece), anywhere),
        vec=(vec, vmem),
        conv_value=(conv_value, vmem),
        conv_select=(conv_select, vmem),
        w_select=(w_select.T, vmem),
        w_step=(w_step.T, vmem),
        w_value=(w_value, anywhere),
        w_gate=(w_gate, anywhere),
        w_out=(w_out, anywhere),
    )
    small_shape = (8, inner + 2 * state)

    def result(shape, kind, spec):
        return (jax.ShapeDtypeStruct(shape, kind), spec)

    outputs = dict(
        o_block=result((total_rows, piece), LOW, vmem),
        o_input=result((total_rows, piece), WIDE, vmem),
        o_small=result(small_shape, WIDE, vmem),
        out_out=result((inner, model), LOW, anywhere),
        out_gate=result((model, inner), LOW, anywhere),
        out_value=result((model, inner), LOW, anywhere),
        out_select=result((state, model), LOW, anywhere),
    )
    link_total = 112 + 16 * dp_axis

    def wide(*shape):
        return pltpu.VMEM(shape, WIDE)

    def low(*shape):
        return pltpu.VMEM(shape, LOW)

    def wide_tokens(lanes, extra=0):
        return wide(seqs, rows + extra, lanes)

    def low_tokens(lanes):
        return low(seqs, rows, lanes)

    def over_of(chunks, depth, columns):
        return low(chunks, dp_axis - 1, depth // (chunks * dp_axis), columns)

    def cut_of(chunks, depth, columns):
        return low(chunks, depth // (chunks * dp_axis), columns)

    semaphores = pltpu.SemaphoreType.DMA
    scratch = dict(
        send_sem=semaphores((link_total,)),
        recv_sem=semaphores((link_total,)),
        load_sem=semaphores((5,)),
        keep_sem=semaphores((7,)),
        v_w_select=low(state, model),
        v_w_value=low(model, inner),
        v_w_gate=low(model, inner),
        v_w_out=low(inner, model),
        gain_all=wide(head_axis, 8, piece),
        x_all=low(head_axis, total_rows, piece),
        cot_all=low(head_axis, total_rows, piece),
        normed=low(total_rows, model),
        inverse=wide(total_rows, state),
        expand=low(state, inner),
        tri=low(rows, rows),
        taps=wide(8, state),
        step_arg=wide_tokens(state),
        step=wide_tokens(state),
        running=wide_tokens(state),
        row_part=wide_tokens(state),
        step_grad=wide_tokens(state),
        sel_keep=wide_tokens(state),
        running_t=wide(seqs, state, rows),
        col_part=wide(seqs, state, rows),
        running_x=wide_tokens(heads * state),
        step_x=wide_tokens(inner),
        scale_x=wide_tokens(inner),
        mixed=wide_tokens(inner),
        inter=wide_tokens(inner),
        projected=wide_tokens(inner),
        act=low_tokens(inner),
        weighted=low_tokens(inner),
        weighted_tail=low_tokens(inner),
        d_mixed_low=low_tokens(inner),
        d_growth=low_tokens(inner),
        value_ext=wide_tokens(inner, RIM),
        select_ext=wide_tokens(state, RIM),
        slope_v=wide_tokens(inner, RIM),
        slope_s=wide_tokens(state, RIM),
        select_own=low_tokens(state),
        select_side=low_tokens(state),
        select_pair=low_tokens(state),
        select_over=low_tokens(state),
        b_all=low_tokens(state),
        c_all=low_tokens(state),
        sel_send=low_tokens(state),
        sel_over=low_tokens(state),
        sel_pair=low_tokens(state),
        sel_side=low_tokens(state),
        gram=wide(seqs, rows, rows),
        pair_weight=wide(seqs, rows, rows),
        state_local=wide(seqs, inner, state),
        decay_row=wide(seqs, inner, state),
        state_in=low(seqs, inner, state),
        state_out=low(seqs, inner, state),
        adj_in=low(seqs, inner, state),
        adj_out=low(seqs, inner, state),
        gate=low(total_rows, inner),
        hidden=low(total_rows, inner),
        gate_low=low(total_rows, inner),
        select_low=low(total_rows, state),
        skip_x=wide(8, inner),
        sums=wide(total_rows, state),
        sum_own=wide(8, total_rows),
        sum_held=wide(head_axis - 1, 8, total_rows),
        mean_own=wide(8, total_rows),
        mean_held=wide(head_axis - 1, 8, total_rows),
        branch=low(head_axis, total_rows, piece),
        sent=low(total_rows, piece),
        branch_near=low(2, total_rows, piece),
        branch_far=low(total_rows, piece),
        normed_near=low(2, total_rows, piece),
        normed_far=low(total_rows, piece),
        small=wide(*small_shape),
        small_mid=wide(*small_shape),
        small_seq=wide(seq_axis - 1, *small_shape),
        small_dp=wide(dp_axis - 1, *small_shape),
        part_gate=low(model, inner),
        part_value=low(model, inner),
        part_select=low(state, model),
        over_out=over_of(2, inner, model),
        over_gate=over_of(2, model, inner),
        over_value=over_of(2, model, inner),
        over_select=over_of(1, state, model),
        up_out=cut_of(2, inner, model),
        up_gate=cut_of(2, model, inner),
        up_value=cut_of(2, model, inner),
        up_select=cut_of(1, state, model),
        mid_out=cut_of(2, inner, model),
        mid_gate=cut_of(2, model, inner),
        mid_value=cut_of(2, model, inner),
        mid_select=cut_of(1, state, model),
    )
    facts = SimpleNamespace(
        names=list(inputs) + list(outputs) + list(scratch),
        seqs=seqs,
        rows=rows,
        heads=heads,
        width=width,
        inner=inner,
        state=state,
        piece=piece,
        head_axis=head_axis,
        seq_axis=seq_axis,
        dp_axis=dp_axis,
        links=link_total,
        norm_at=starts[2],
        select_at=starts[3],
        bias_at=starts[4],
        decay_at=starts[5],
        skip_at=starts[6],
    )
    results = pl.pallas_call(
        functools.partial(mixer_kernel, facts),
        out_shape=[shape for shape, _ in outputs.values()],
        in_specs=[spec for _, spec in inputs.values()],
        out_specs=[spec for _, spec in outputs.values()],
        scratch_shapes=list(scratch.values()),
        compiler_params=pltpu.CompilerParams(
            collective_id=0, has_side_effects=True, vmem_limit_bytes=67043328
        ),
    )(*[value for value, _ in inputs.values()])
    got = SimpleNamespace(**dict(zip(outputs, results, strict=True)))
    steps = 8

    def by_rows(depth, columns):
        return pl.BlockSpec((depth // steps, columns), lambda i: (i, 0))

    def whole(*shape):
        return pl.BlockSpec(shape, lambda i: (0, 0))

    streamed = [(total_rows, piece), (total_rows, piece), (inner, model), (model, inner), (model, inner)]
    kinds = [LOW, WIDE, WIDE, WIDE, WIDE]
    fixed = [
        (half, model),
        (heads, model),
        (1, piece),
        (4, inner),
        (1, inner),
        (4, half),
        (1, half),
        (1, heads),
        (1, heads),
        (1, heads),
        (1, inner),
    ]
    final = pl.pallas_call(
        functools.partial(finish_kernel, half, heads, piece, inner),
        grid=(steps,),
        out_shape=[jax.ShapeDtypeStruct(shape, kind) for shape, kind in zip(streamed, kinds)]
        + [jax.ShapeDtypeStruct(shape, WIDE) for shape in fixed],
        in_specs=[by_rows(*shape) for shape in streamed]
        + [whole(state, model), whole(*small_shape)],
        out_specs=[by_rows(*shape) for shape in streamed] + [whole(*shape) for shape in fixed],
    )(
        got.o_block,
        got.o_input,
        got.out_out,
        got.out_gate,
        got.out_value,
        got.out_select,
        got.o_small,
    )
    block_output, input_grad, g_out, g_gate, g_value, g_select, g_step = final[:7]
    g_norm, g_conv, g_bias, g_conv_s, g_bias_s, g_step_bias, g_decay, g_skip, g_gain = final[7:]
    return (
        block_output.reshape(seqs, rows, piece),
        input_grad.reshape(seqs, rows, piece),
        g_norm[0],
        g_gate,
        g_value,
        g_select.T,
        g_step.T,
        g_conv,
        g_bias[0],
        g_conv_s,
        g_bias_s[0],
        g_step_bias[0],
        g_decay[0],
        g_skip[0],
        g_gain[0],
        g_out,
    )


def solution(mesh):
    columns, single, tokens = P(None, HEAD), P(HEAD), P(DP, SEQ, HEAD)
    in_specs = (
        tokens,
        single,
        columns,
        columns,
        columns,
        columns,
        columns,
        single,
        columns,
        single,
        single,
        single,
        single,
        single,
        P(HEAD, None),
        tokens,
    )
    out_specs = (
        tokens,
        tokens,
        single,
        columns,
        columns,
        columns,
        columns,
        columns,
        single,
        columns,
        single,
        single,
        single,
        single,
        single,
        P(HEAD, None),
    )
    return jax.shard_map(
        functools.partial(body, dict(mesh.shape)),
        mesh=mesh,
        in_specs=in_specs,
        out_specs=out_specs,
        check_vma=False,
    )
```

time: 903 us -> 251 us (0.28); the launches traced: 890 us -> 250 us
  waiting for transfers between devices: 572 us -> 0 us
  Pallas kernels: 0 us -> 241 us
  matrix products: 99 us -> 0 us
  blocking collectives: 72.8 us -> 0 us
  local copies, waits for them, and re-layouts: 70 us -> 4.64 us
  other arithmetic: 51.2 us -> 4.53 us
  between operations: 16.2 us -> 0.67 us
  starting transfers between devices: 9.16 us -> 0 us
    psum x2 -> x0, waiting for transfers between devices: 485 us -> none  [the longest x1 416 us: body(): lax.psum((grad_norm_gain, grad_w_gate, grad_w_value, grad_w_select, grad_...]
    pallas_call x0 -> x2, Pallas kernels: none -> 241 us  [the longest x1 230 us: body(): pl.pallas_call(functools.partial(mixer_kernel, facts), out_shape=[shape f...]
    dot_general x33 -> x0, matrix products: 99 us -> none  [the longest x2 11.7 us: block_backward(): jnp.einsum('qth,qhp->thp', mixing, grad_block, precision=HIGHEST)]
    all_gather x4 -> x0, waiting for transfers between devices: 75.2 us -> none  [the longest x2 62.4 us: carried_in(): pieces = jax.tree.map(lambda part: lax.all_gather(part, axis), value)]
    psum x3 -> x0, blocking collectives: 47.9 us -> none  [the longest x1 35.1 us: body(): lax.psum((grad_norm_gain, grad_w_gate, grad_w_value, grad_w_select, grad_...]
    all_gather x3 -> x0, blocking collectives: 24.9 us -> none  [the longest x1 13.9 us: carried_in(): pieces = jax.tree.map(lambda part: lax.all_gather(part, axis), value)]
    reduce_sum x9 -> x0, other arithmetic: 22.9 us -> none  [the longest x2 7.16 us: filter_back(): return (grad_pre, jnp.stack(weight_rows), jnp.sum(slope_grad, axis=(0, 1)))]
    unnamed x184 -> x5, local copies, waits for them, and re-layouts: 23.4 us -> 3.37 us
  transfers between devices with their start and end apart: 12 -> 0, of which waited for: 6 -> 0; matrix products, arithmetic and copies ran while one was open for 16% -> 0% of each run, Pallas kernels for 0% -> 0%
where the time goes in v1:
time: 251 us; the launch traced here: 250 us
  Pallas kernels  241 us (96%)
  local copies, waits for them, and re-layouts  4.64 us (2%)
  other arithmetic  4.53 us (2%)
    pallas_call x1, Pallas kernels, body(): pl.pallas_call(functools.partial(mixer_kernel, facts), out_shape=[shape f...  230 us
    pallas_call x1, Pallas kernels, body(): pl.pallas_call(functools.partial(finish_kernel, half, heads, piece, inner...  10.7 us

profile of v1, /device:TPU:24, one launch (start us, length us, event | category | flops | bytes accessed | tf_op | source)
XLA Modules:
  0.0 250.4 jit_solution(11725387251528459957)
XLA Ops:
  0.7 0.7 constant_dynamic-update-slice_fusion.6
  1.3 0.7 constant_dynamic-update-slice_fusion.5
  2.0 0.7 constant_dynamic-update-slice_fusion.4
  2.7 0.7 constant_dynamic-update-slice_fusion.3
  3.4 0.7 constant_dynamic-update-slice_fusion.2
  4.0 0.7 constant_dynamic-update-slice_fusion.1
  4.7 0.7 constant_dynamic-update-slice_fusion
  5.4 0.6 broadcast_in_dim.3.refs_2_
  6.0 229.9 %shard_map.279 = (bf16[512,384]{1,0:T(8,128)(2,1)}, f32[512,384]{1,0:T(8,128)}, f32[8,1024]{1,0:T(8,128)}, bf16[768,1536]{1,0:T(8,128)(2,1)}, bf16[1536,768]{1,0...) custom-call(bf16[512,384]{1,0:T(8,128)(2,1)} %bitcast.12, bf16[512,384]{1,0:T(8,128)(2,1)} %bitcast.13, ...), custom_call_target="tpu_custom_call" | custom-call | tf_op jit(solution)/shard_map/pallas_call | solution.py:1194
  235.9 10.7 %shard_map.280 = (bf16[512,384]{1,0:T(8,128)(2,1)}, f32[512,384]{1,0:T(8,128)}, f32[768,1536]{1,0:T(8,128)}, f32[1536,768]{1,0:T(8,128)}, f32[1536,768]{1,0:T(8,...) custom-call(bf16[512,384]{1,0:T(8,128)(2,1)} %get-tuple-element.39.r, ...), custom_call_target="tpu_custom_call" | custom-call | tf_op jit(solution)/shard_map/pallas_call | solution.py:1228
  246.6 1.3 reduce
  247.9 1.3 reduce.1
  249.1 1.3 reduce.2
  (1 shorter events, 0.0 us)

commit v2 on v1

--- a/solution.py
+++ b/solution.py
@@ -134,7 +134,7 @@
         for copy in copies:
             copy.wait_send()
 
-    r.gain_all[h] = jnp.broadcast_to(r.vec[0:1, size.norm_at : size.norm_at + piece], (8, piece))
+    r.gain_all[h] = jnp.broadcast_to(r.norm_gain[...][None].astype(WIDE), (8, piece))
     gain_copies = gather_start(r.gain_all.at[h], r.gain_all)
     input_copies = gather_start(r.x, r.x_all)
     cot_copies = gather_start(r.cot, r.cot_all)
@@ -152,11 +152,14 @@
     r.tri[...] = jnp.where(lower, 1.0, 0.0).astype(LOW)
     shift = jnp.where(iota((half, state), 0) + place == iota((half, state), 1), 1.0, 0.0).astype(LOW)
     r.taps[0:4, :] = picked(r.conv_select[...], shift)
-    few = jnp.broadcast_to(r.vec[0:1, size.select_at : size.select_at + half], (8, half))
+    few = jnp.broadcast_to(r.bias_select[...][None], (8, half))
     r.taps[4:5, :] = picked(few, shift)[0:1, :]
-    for row, start in enumerate((size.bias_at, size.decay_at, size.skip_at)):
-        low_lanes = jnp.broadcast_to(r.vec[0:1, start : start + state], (8, state))
-        r.taps[5 + row : 6 + row, :] = jnp.where(odd, low_lanes, pltpu.roll(low_lanes, half, 1))[0:1, :]
+    moved = jnp.where(
+        iota((heads, state), 0) + spare == iota((heads, state), 1), 1.0, 0.0
+    ).astype(LOW)
+    for row, source in enumerate((r.step_bias, r.decay_log, r.skip_gain)):
+        few = jnp.broadcast_to(source[...][None], (8, heads))
+        r.taps[5 + row : 6 + row, :] = picked(few, moved)[0:1, :]
     r.v_w_select[...] = jnp.zeros((state, model), LOW)
     r.v_w_select[pl.ds(pl.multiple_of(place, half), half), :] = r.w_select[...]
     padded = jnp.concatenate([r.w_step[...], jnp.zeros((16 - heads, model), LOW)], axis=0)
@@ -197,6 +200,26 @@
 
     lax.fori_loop(0, total_rows // 64, norm_rows, 0)
 
+    paired = dp_count == 2
+    mate = {DP: lax.rem(d + 1, dp_count)}
+    wide_half = model // 2
+    own_half = pl.ds(pl.multiple_of(lax.rem(d, 2) * wide_half, 128), wide_half)
+    mate_half = pl.ds(pl.multiple_of(lax.rem(d + 1, 2) * wide_half, 128), wide_half)
+    halves = head_count // 2
+
+    def chunk_sends(source, target):
+        chunks, _, lanes = target.shape
+        copies = []
+        for c in range(chunks):
+            at = slice(c * lanes, (c + 1) * lanes)
+            copies.append(links.copy(source.at[:, at], target.at[c], mate))
+            copies[-1].start()
+        return copies
+
+    if paired:
+        send_normed = links.copy(r.normed.at[:, mate_half], r.far_normed, mate)
+        send_normed.start()
+
     for q in range(seqs):
         at = pl.ds(q * rows, rows)
         both = product(r.normed[at, :], r.v_w_select[...], 1, 1)
@@ -241,11 +264,14 @@
         r.running_t[q] = picked(fall, tri[...], 0, 1)
 
         def spread(g, _):
-            pick = jnp.where(iota((state, state), 0) == spare + g, 1.0, 0.0).astype(LOW)
-            r.running_x[q, :, block(g * state, state)] = picked(r.running[q], pick)
+            lanes = 4 * state
+            pick = jnp.where(
+                iota((state, lanes), 0) == spare + 4 * g + iota((state, lanes), 1) // state, 1.0, 0.0
+            ).astype(LOW)
+            r.running_x[q, :, block(g * lanes, lanes)] = picked(r.running[q], pick)
             return 0
 
-        lax.fori_loop(0, heads, spread, 0)
+        lax.fori_loop(0, heads // 4, spread, 0)
         r.step_x[q] = picked(step, r.expand[...], count=2)
         last = running[rows - 1 : rows, :]
         r.scale_x[q] = picked(jnp.exp(last - running), r.expand[...], count=2)
@@ -272,7 +298,7 @@
             total = total + taps[k : k + 1, :] * wide[RIM - 3 + k : RIM - 3 + k + count]
         return total
 
-    value_bias, gate_gain = r.vec[0:1, 0:inner], r.vec[0:1, inner : 2 * inner]
+    value_bias, gate_gain = r.bias_value[...][None], r.gate_gain[...][None]
 
     for q in range(seqs):
         conv = convolve(r.select_ext, q, 0, rows, r.taps, r.taps[4:5, :])
@@ -304,6 +330,12 @@
 
     lax.fori_loop(0, seqs, gate_matmul, 0)
     swap.wait()
+    gather_end(cot_copies)
+    own_cot.wait()
+    if paired:
+        at = pl.ds(lax.rem(d + 1, 2) * halves, halves)
+        send_cot = links.copy(r.cot_all.at[at], r.far_cot, mate)
+        send_cot.start()
     upper = h >= 2
     first, second = r.select_pair[...], r.select_over[...]
     r.b_all[...] = jnp.where(upper, second, first)
@@ -379,8 +411,6 @@
         return 0
 
     lax.fori_loop(0, pair_total, forward_slot, 0)
-    gather_end(cot_copies)
-    own_cot.wait()
     loads[2].wait()
 
     def d_hidden_matmul(q, _):
@@ -489,78 +519,96 @@
     skip_total = jnp.broadcast_to(jnp.sum(skip_total, axis=0, keepdims=True), (8, inner))
     small[2:3, lanes] = picked(skip_total, r.expand[...], 1, 1)[0:1, :]
 
+    if paired:
+        send_hidden = chunk_sends(r.hidden, r.far_hidden)
+        send_gate = chunk_sends(r.gate_low, r.far_gate)
+
     for q in range(seqs):
         r.state_local[q] = product(r.d_growth[q], r.c_all[q], 0, 0)
 
     ends = (s == 0) | (s == seq_count - 1)
     inside = (s > 0) & (s < seq_count - 1)
 
-    def rows_of(me, p):
-        return pl.ds(pl.multiple_of((me.chunk * dp_count + p) * me.depth, 16), me.depth)
+    keeps = []
+
+    def stream_links(own, up, mid, target):
+        me = SimpleNamespace(own=own, up=up, mid=mid, copies=[])
+        me.copy_up = links.copy(own, up, {SEQ: s ^ 1})
+        me.copy_mid = links.copy(own, mid, {SEQ: seq_count - 1 - s})
+        me.copy_down = links.copy(up, up, {SEQ: s ^ 1})
+        me.keep = pltpu.make_async_copy(up, target, r.keep_sem.at[len(keeps)])
+        me.copies_out = [
+            links.copy(up, target, {DP: lax.rem(d + j, dp_count)}) for j in range(1, dp_count)
+        ]
+        keeps.append(me)
+        return me
 
     def stream_start(bufs, chunk):
         part, over, up, mid, out = bufs
-        me = SimpleNamespace(part=part, out=out, chunk=chunk, depth=up.shape[1])
-        me.over, me.up, me.mid = over.at[chunk], up.at[chunk], mid.at[chunk]
-        own = part.at[rows_of(me, d), :]
-        me.copies = []
+        depth = up.shape[1]
+
+        def rows_of(p):
+            return pl.ds(pl.multiple_of((chunk * dp_count + p) * depth, 16), depth)
+
+        me = stream_links(part.at[rows_of(d), :], up.at[chunk], mid.at[chunk], out.at[rows_of(d), :])
+        me.over = over.at[chunk]
         for j in range(1, dp_count):
             to = lax.rem(d + j, dp_count)
-            copy = links.copy(part.at[rows_of(me, to), :], me.over.at[j - 1], {DP: to})
+            copy = links.copy(part.at[rows_of(to), :], me.over.at[j - 1], {DP: to})
             copy.start()
             me.copies.append(copy)
-        me.copy_up = links.copy(own, me.up, {SEQ: s ^ 1})
-        me.copy_mid = links.copy(own, me.mid, {SEQ: seq_count - 1 - s})
-        me.copy_down = links.copy(me.up, me.up, {SEQ: s ^ 1})
-        target = out.at[rows_of(me, d), :]
-        me.keep = pltpu.make_async_copy(me.up, target, r.keep_sem.at[len(keeps)])
-        keeps.append(me)
-        me.copies_out = [
-            links.copy(me.up, target, {DP: lax.rem(d + j, dp_count)}) for j in range(1, dp_count)
-        ]
         return me
 
-    keeps = []
-
-    def add_rows(me, target, terms):
-        depth = me.depth
+    def pair_streams(part, up, mid, out, by_columns):
+        made = []
+        for chunk in range(up.shape[0]):
+            if by_columns:
+                depth = up.shape[1]
+                target = out.at[chunk * depth : (chunk + 1) * depth, own_half]
+            else:
+                lanes = up.shape[2]
+                first = pl.multiple_of(lax.rem(d, 2) * wide_half, 16)
+                target = out.at[pl.ds(first, wide_half), chunk * lanes : (chunk + 1) * lanes]
+            made.append(stream_links(part.at[chunk], up.at[chunk], mid.at[chunk], target))
+        return made
+
+    def add_rows(first, target, terms):
+        depth = target.shape[0]
         step = next(t for t in (64, 48, 16) if depth % t == 0)
 
         def add(i, _):
             at = pl.ds(pl.multiple_of(i * step, 16), step)
-            own = pl.ds(pl.multiple_of((me.chunk * dp_count + d) * depth + i * step, 16), step)
-            total = me.part[own, :].astype(WIDE)
+            total = first[at, :].astype(WIDE)
             for term in terms:
                 total = total + term[at, :].astype(WIDE)
-            if target is None:
-                me.part[own, :] = total.astype(LOW)
-            else:
-                target[at, :] = total.astype(LOW)
+            target[at, :] = total.astype(LOW)
             return 0
 
         lax.fori_loop(0, depth // step, add, 0)
+
+    def stream_up(me):
+        @pl.when(ends)
+        def _():
+            me.copy_up.start()
 
     def stream_a(me):
         for copy in me.copies:
             copy.wait_recv()
-        add_rows(me, None, [me.over.at[j] for j in range(dp_count - 1)])
-
-        @pl.when(ends)
-        def _():
-            me.copy_up.start()
+        add_rows(me.own, me.own, [me.over.at[j] for j in range(dp_count - 1)])
+        stream_up(me)
 
     def stream_b(me):
         @pl.when(inside)
         def _():
             me.copy_up.wait_recv()
-            add_rows(me, None, [me.up])
+            add_rows(me.own, me.own, [me.up])
             me.copy_mid.start()
 
     def stream_c(me):
         @pl.when(inside)
         def _():
             me.copy_mid.wait_recv()
-            add_rows(me, me.up, [me.mid])
+            add_rows(me.own, me.up, [me.mid])
             me.copy_down.start()
 
         @pl.when(ends)
@@ -587,17 +635,47 @@
             me.copy_mid.wait_send()
             me.copy_down.wait_send()
 
+    def pair_grad(part, right, far_right, sends, made):
+        lanes = part.shape[2]
+        for c, copy in enumerate(sends):
+            copy.wait()
+            at = slice(c * lanes, (c + 1) * lanes)
+            for start in range(0, wide_half, piece):
+                first = lax.rem(d, 2) * wide_half + start
+                left = r.normed[:, pl.ds(pl.multiple_of(first, 128), piece)]
+                total = product(left, right[:, at], 0, 0)
+                total = total + product(r.far_normed[:, start : start + piece], far_right[c], 0, 0)
+                part[c, start : start + piece, :] = total.astype(LOW)
+            stream_up(made[c])
+
+    def out_grad():
+        for c, copy in enumerate(send_hidden):
+            copy.wait_recv()
+            lanes = r.far_hidden.shape[2]
+            for k in range(halves):
+                left = r.hidden[:, c * lanes : (c + 1) * lanes]
+                total = product(left, r.cot_all[lax.rem(d, 2) * halves + k], 0, 0)
+                total = total + product(r.far_hidden[c], r.far_cot[k], 0, 0)
+                r.part_out[c, :, k * piece : (k + 1) * piece] = total.astype(LOW)
+            stream_up(out_streams[c])
+
     def big_grad(part, left, right, lanes):
         for start in range(0, part.shape[0], lanes):
             columns = slice(start, start + lanes)
             part[columns, :] = product(left[:, columns], right, 0, 0).astype(LOW)
 
-    bufs_gate = (r.part_gate, r.over_gate, r.up_gate, r.mid_gate, r.out_gate)
-    bufs_out = (r.v_w_out, r.over_out, r.up_out, r.mid_out, r.out_out)
-    bufs_value = (r.part_value, r.over_value, r.up_value, r.mid_value, r.out_value)
-    bufs_select = (r.part_select, r.over_select, r.up_select, r.mid_select, r.out_select)
-    big_grad(r.part_gate, r.normed, r.gate_low[...], piece)
-    gate_streams = [stream_start(bufs_gate, c) for c in range(r.up_gate.shape[0])]
+    if paired:
+        out_streams = pair_streams(r.part_out, r.up_out, r.mid_out, r.out_out, True)
+        gate_streams = pair_streams(r.part_gate, r.up_gate, r.mid_gate, r.out_gate, False)
+        value_streams = pair_streams(r.part_value, r.up_value, r.mid_value, r.out_value, False)
+        select_streams = pair_streams(r.part_select, r.up_select, r.mid_select, r.out_select, True)
+    else:
+        bufs_gate = (r.part_gate, r.over_gate, r.up_gate, r.mid_gate, r.out_gate)
+        bufs_out = (r.part_out, r.over_out, r.up_out, r.mid_out, r.out_out)
+        bufs_value = (r.part_value, r.over_value, r.up_value, r.mid_value, r.out_value)
+        bufs_select = (r.part_select, r.over_select, r.up_select, r.mid_select, r.out_select)
+        big_grad(r.part_gate, r.normed, r.gate_low[...], piece)
+        gate_streams = [stream_start(bufs_gate, c) for c in range(r.up_gate.shape[0])]
 
     def spread_parts(part, near):
         copies = [
@@ -631,10 +709,11 @@
             r.hidden[...], r.v_w_out[:, k * piece : (k + 1) * piece]
         ).astype(LOW)
     branch_copies = spread_parts(r.branch, r.branch_near)
-    for k in range(head_count):
-        columns = slice(k * piece, (k + 1) * piece)
-        r.v_w_out[:, columns] = product(r.hidden[...], r.cot_all[k], 0, 0).astype(LOW)
-    out_streams = [stream_start(bufs_out, c) for c in range(r.up_out.shape[0])]
+    if not paired:
+        for k in range(head_count):
+            columns = slice(k * piece, (k + 1) * piece)
+            r.part_out[:, columns] = product(r.hidden[...], r.cot_all[k], 0, 0).astype(LOW)
+        out_streams = [stream_start(bufs_out, c) for c in range(r.up_out.shape[0])]
 
     r.pair_weight[...] = jnp.zeros((seqs, rows, rows), WIDE)
     r.row_part[...] = jnp.zeros((seqs, rows, state), WIDE)
@@ -685,11 +764,17 @@
 
     slots = chunk_total + 2 * (seq_count - 1)
     assert slots <= pair_total, slots
-    lax.fori_loop(0, 5, backward_slot, 0)
+    lax.fori_loop(0, chunk_total, backward_slot, 0)
     branch_last = spread_over(r.branch, r.branch_near, r.sent, r.branch_far, branch_copies)
-    lax.fori_loop(5, 8, backward_slot, 0)
-    stream_a(gate_streams[0])
-    lax.fori_loop(8, pair_total, backward_slot, 0)
+    if paired:
+        send_normed.wait()
+        send_cot.wait()
+
+        @pl.when(s == 0)
+        def _():
+            out_grad()
+
+    lax.fori_loop(chunk_total, pair_total, backward_slot, 0)
 
     for q in range(seqs):
         pairs = r.pair_weight[q].astype(LOW)
@@ -737,6 +822,12 @@
     def _():
         for copy in rim_back:
             copy.start()
+
+    if paired:
+
+        @pl.when(s > 0)
+        def _():
+            out_grad()
 
     sel_over.wait()
     r.sel_pair[...] = (r.sel_keep[...] + r.sel_over[...].astype(WIDE)).astype(LOW)
@@ -797,10 +888,21 @@
     totals = lax.fori_loop(0, total_rows // tile, conv_back, (blank,) * 5)
     for k in range(5):
         small[k : k + 1, 0:inner] = jnp.sum(totals[k], axis=0, keepdims=True)
-    big_grad(r.part_value, r.normed, r.gate[...], piece)
-    value_streams = [stream_start(bufs_value, c) for c in range(r.up_value.shape[0])]
-    stream_a(gate_streams[1])
-    stream_b(gate_streams[0])
+    if paired:
+        send_value = chunk_sends(r.gate, r.far_value)
+        stream_b(out_streams[0])
+        stream_b(out_streams[1])
+        pair_grad(r.part_gate, r.gate_low, r.far_gate, send_gate, gate_streams)
+    else:
+        big_grad(r.part_value, r.normed, r.gate[...], piece)
+        value_streams = [stream_start(bufs_value, c) for c in range(r.up_value.shape[0])]
+        for me in out_streams + gate_streams:
+            stream_a(me)
+        stream_b(out_streams[0])
+        stream_b(out_streams[1])
+    stream_c(out_streams[0])
+    stream_b(out_streams[2])
+    stream_c(out_streams[1])
 
     for q in range(seqs):
         step = r.step[q]
@@ -846,9 +948,27 @@
             )
         small[4:5, at] += jnp.sum(own, axis=0, keepdims=True)
         r.select_low[pl.ds(q * rows, rows), :] = jnp.where(mine, grad, r.step_grad[q]).astype(LOW)
-    big_grad(r.part_select, r.select_low, r.normed[...], state)
-    select_stream = stream_start(bufs_select, 0)
-    stream_a(out_streams[0])
+    if paired:
+        send_select = links.copy(r.select_low, r.far_select, mate)
+        send_select.start()
+    else:
+        big_grad(r.part_select, r.select_low, r.normed[...], state)
+        select_streams = [stream_start(bufs_select, 0)]
+    stream_b(gate_streams[0])
+    stream_c(out_streams[2])
+
+    if paired:
+        pair_grad(r.part_value, r.gate, r.far_value, send_value, value_streams)
+        send_select.wait()
+        total = product(r.select_low[...], r.normed[:, own_half], 0, 0)
+        total = total + product(r.far_select[...], r.far_normed[...], 0, 0)
+        r.part_select[0] = total.astype(LOW)
+        stream_up(select_streams[0])
+        for copy in send_hidden:
+            copy.wait_send()
+    else:
+        for me in value_streams + select_streams:
+            stream_a(me)
     stream_b(gate_streams[1])
     stream_c(gate_streams[0])
 
@@ -888,9 +1008,9 @@
         lax.fori_loop(0, seqs, d_normed_rows, 0)
     normed_copies = spread_parts(r.branch, r.normed_near)
     mean_copies = row_sums(r.mean_own, r.mean_held)
-    stream_a(out_streams[1])
-    stream_b(out_streams[0])
+    stream_b(gate_streams[2])
     stream_c(gate_streams[1])
+    stream_b(value_streams[0])
     normed_last = spread_over(r.branch, r.normed_near, r.sent, r.normed_far, normed_copies)
     row_sums_end(r.mean_own, r.mean_held, mean_copies)
     normed_last.wait()
@@ -923,18 +1043,14 @@
         copy = links.copy(small, r.small_seq.at[j - 1], {SEQ: lax.rem(s + j, seq_count)})
         copy.start()
         small_copies.append(copy)
-    stream_a(value_streams[0])
-    stream_b(out_streams[1])
-    stream_c(out_streams[0])
-    stream_a(value_streams[1])
-    stream_b(value_streams[0])
-    stream_c(out_streams[1])
-    stream_a(select_stream)
+    stream_c(gate_streams[2])
     stream_b(value_streams[1])
-    stream_b(select_stream)
     stream_c(value_streams[0])
+    stream_b(value_streams[2])
     stream_c(value_streams[1])
-    stream_c(select_stream)
+    stream_b(select_streams[0])
+    stream_c(value_streams[2])
+    stream_c(select_streams[0])
     total = small[...]
     for j, copy in enumerate(small_copies):
         copy.wait()
@@ -980,14 +1096,14 @@
         low_rows, high_rows = matrix[0:half, :].astype(WIDE), matrix[half : 2 * half, :].astype(WIDE)
         g_select[...] = jnp.where(odd, high_rows, low_rows)
         g_step[...] = jnp.where(odd, low_rows, high_rows)[0:heads, :]
-        g_norm[...] = small[7:8, 0:piece]
+        g_norm[...] = small[7, 0:piece]
         g_conv[...] = small[0:4, 0:inner]
-        g_bias[...] = small[4:5, 0:inner]
-        g_gain[...] = small[5:6, 0:inner]
+        g_bias[...] = small[4, 0:inner]
+        g_gain[...] = small[5, 0:inner]
         g_conv_s[...] = small[0:4, inner : inner + half]
-        g_bias_s[...] = small[4:5, inner : inner + half]
+        g_bias_s[...] = small[4, inner : inner + half]
         for row, target in enumerate((g_bias_h, g_decay, g_skip)):
-            target[...] = small[row : row + 1, inner + 2 * half : inner + 2 * half + heads]
+            target[...] = small[row, inner + 2 * half : inner + 2 * half + heads]
 
 
 def body(size, *args):
@@ -1019,22 +1135,18 @@
     total_rows = seqs * rows
     assert head_axis == 4 and seq_axis == 4 and 2 * half == state and heads <= half and 2 * width == state
 
-    def aligned(values):
-        values = values.astype(WIDE)
-        return jnp.pad(values, (0, -values.shape[0] % state))
-
-    singles = (bias_value, gate_gain, norm_gain, bias_select, step_bias, decay_log, skip_gain)
-    singles = [aligned(values) for values in singles]
-    starts = [0]
-    for values in singles:
-        starts.append(starts[-1] + values.shape[0])
-    vec = jnp.concatenate(singles)[None]
     vmem = pl.BlockSpec(memory_space=pltpu.VMEM)
     anywhere = pl.BlockSpec(memory_space=pl.ANY)
     inputs = dict(
         x=(block_input.reshape(total_rows, piece), anywhere),
         cot=(out_cotangent.reshape(total_rows, piece), anywhere),
-        vec=(vec, vmem),
+        bias_value=(bias_value, vmem),
+        gate_gain=(gate_gain, vmem),
+        norm_gain=(norm_gain, vmem),
+        bias_select=(bias_select, vmem),
+        step_bias=(step_bias, vmem),
+        decay_log=(decay_log, vmem),
+        skip_gain=(skip_gain, vmem),
         conv_value=(conv_value, vmem),
         conv_select=(conv_select, vmem),
         w_select=(w_select.T, vmem),
@@ -1057,7 +1169,7 @@
         out_value=result((model, inner), LOW, anywhere),
         out_select=result((state, model), LOW, anywhere),
     )
-    link_total = 112 + 16 * dp_axis
+    link_total = 128 + 16 * dp_axis
 
     def wide(*shape):
         return pltpu.VMEM(shape, WIDE)
@@ -1082,7 +1194,7 @@
         send_sem=semaphores((link_total,)),
         recv_sem=semaphores((link_total,)),
         load_sem=semaphores((5,)),
-        keep_sem=semaphores((7,)),
+        keep_sem=semaphores((10,)),
         v_w_select=low(state, model),
         v_w_value=low(model, inner),
         v_w_gate=low(model, inner),
@@ -1156,22 +1268,47 @@
         small_mid=wide(*small_shape),
         small_seq=wide(seq_axis - 1, *small_shape),
         small_dp=wide(dp_axis - 1, *small_shape),
-        part_gate=low(model, inner),
-        part_value=low(model, inner),
-        part_select=low(state, model),
-        over_out=over_of(2, inner, model),
-        over_gate=over_of(2, model, inner),
-        over_value=over_of(2, model, inner),
-        over_select=over_of(1, state, model),
-        up_out=cut_of(2, inner, model),
-        up_gate=cut_of(2, model, inner),
-        up_value=cut_of(2, model, inner),
-        up_select=cut_of(1, state, model),
-        mid_out=cut_of(2, inner, model),
-        mid_gate=cut_of(2, model, inner),
-        mid_value=cut_of(2, model, inner),
-        mid_select=cut_of(1, state, model),
     )
+    if dp_axis == 2:
+        scratch.update(
+            far_normed=low(total_rows, model // 2),
+            far_cot=low(head_axis // 2, total_rows, piece),
+            far_hidden=low(3, total_rows, inner // 3),
+            far_gate=low(3, total_rows, inner // 3),
+            far_value=low(3, total_rows, inner // 3),
+            far_select=low(total_rows, state),
+            part_out=low(3, inner // 3, model // 2),
+            part_gate=low(3, model // 2, inner // 3),
+            part_value=low(3, model // 2, inner // 3),
+            part_select=low(1, state, model // 2),
+            up_out=low(3, inner // 3, model // 2),
+            mid_out=low(3, inner // 3, model // 2),
+            up_gate=low(3, model // 2, inner // 3),
+            mid_gate=low(3, model // 2, inner // 3),
+            up_value=low(3, model // 2, inner // 3),
+            mid_value=low(3, model // 2, inner // 3),
+            up_select=low(1, state, model // 2),
+            mid_select=low(1, state, model // 2),
+        )
+    else:
+        scratch.update(
+            part_out=low(inner, model),
+            part_gate=low(model, inner),
+            part_value=low(model, inner),
+            part_select=low(state, model),
+            over_out=over_of(3, inner, model),
+            over_gate=over_of(3, model, inner),
+            over_value=over_of(3, model, inner),
+            over_select=over_of(1, state, model),
+            up_out=cut_of(3, inner, model),
+            up_gate=cut_of(3, model, inner),
+            up_value=cut_of(3, model, inner),
+            up_select=cut_of(1, state, model),
+            mid_out=cut_of(3, inner, model),
+            mid_gate=cut_of(3, model, inner),
+            mid_value=cut_of(3, model, inner),
+            mid_select=cut_of(1, state, model),
+        )
     facts = SimpleNamespace(
         names=list(inputs) + list(outputs) + list(scratch),
         seqs=seqs,
@@ -1185,11 +1322,6 @@
         seq_axis=seq_axis,
         dp_axis=dp_axis,
         links=link_total,
-        norm_at=starts[2],
-        select_at=starts[3],
-        bias_at=starts[4],
-        decay_at=starts[5],
-        skip_at=starts[6],
     )
     results = pl.pallas_call(
         functools.partial(mixer_kernel, facts),
@@ -1202,28 +1334,28 @@
         ),
     )(*[value for value, _ in inputs.values()])
     got = SimpleNamespace(**dict(zip(outputs, results, strict=True)))
-    steps = 8
+    steps = 4
 
     def by_rows(depth, columns):
         return pl.BlockSpec((depth // steps, columns), lambda i: (i, 0))
 
     def whole(*shape):
-        return pl.BlockSpec(shape, lambda i: (0, 0))
+        return pl.BlockSpec(shape, lambda i: (0,) * len(shape))
 
     streamed = [(total_rows, piece), (total_rows, piece), (inner, model), (model, inner), (model, inner)]
     kinds = [LOW, WIDE, WIDE, WIDE, WIDE]
     fixed = [
         (half, model),
         (heads, model),
-        (1, piece),
+        (piece,),
         (4, inner),
-        (1, inner),
+        (inner,),
         (4, half),
-        (1, half),
-        (1, heads),
-        (1, heads),
-        (1, heads),
-        (1, inner),
+        (half,),
+        (heads,),
+        (heads,),
+        (heads,),
+        (inner,),
     ]
     final = pl.pallas_call(
         functools.partial(finish_kernel, half, heads, piece, inner),
@@ -1247,19 +1379,19 @@
     return (
         block_output.reshape(seqs, rows, piece),
         input_grad.reshape(seqs, rows, piece),
-        g_norm[0],
+        g_norm,
         g_gate,
         g_value,
         g_select.T,
         g_step.T,
         g_conv,
-        g_bias[0],
+        g_bias,
         g_conv_s,
-        g_bias_s[0],
-        g_step_bias[0],
-        g_decay[0],
-        g_skip[0],
-        g_gain[0],
+        g_bias_s,
+        g_step_bias,
+        g_decay,
+        g_skip,
+        g_gain,
         g_out,
     )
 

time: 251 us -> 216 us (0.86)
  Pallas kernels: 241 us -> 214 us
  local copies, waits for them, and re-layouts: 4.64 us -> 0 us
  other arithmetic: 4.53 us -> 0 us
    pallas_call x1, Pallas kernels: 230 us -> 204 us  [body(): pl.pallas_call(functools.partial(mixer_kernel, facts), out_shape=[shape f...]
    pallas_call x3 -> x0, other arithmetic: 3.84 us -> none  [body(): pl.pallas_call(functools.partial(finish_kernel, half, heads, piece, inner...]
    unnamed x5 -> x0, local copies, waits for them, and re-layouts: 3.37 us -> none
where the time goes in v2:
time: 216 us; the launch traced here: 215 us
  Pallas kernels  214 us (99%)
    pallas_call x1, Pallas kernels, body(): pl.pallas_call(functools.partial(mixer_kernel, facts), out_shape=[shape f...  204 us
    pallas_call x1, Pallas kernels, body(): pl.pallas_call(functools.partial(finish_kernel, half, heads, piece, inner...  9.89 us

profile of v2, /device:TPU:24, one launch (start us, length us, event | category | flops | bytes accessed | tf_op | source)
XLA Modules:
  0.0 214.6 jit_solution(7134721906626339649)
XLA Ops:
  0.7 203.9 %shard_map.279 = (bf16[512,384]{1,0:T(8,128)(2,1)}, f32[512,384]{1,0:T(8,128)}, f32[8,1024]{1,0:T(8,128)}, bf16[768,1536]{1,0:T(8,128)(2,1)}, bf16[1536,768]{1,0...) custom-call(bf16[512,384]{1,0:T(8,128)(2,1)} %bitcast.8, bf16[512,384]{1,0:T(8,128)(2,1)} %bitcast.9, ...), custom_call_target="tpu_custom_call" | custom-call | tf_op jit(solution)/shard_map/pallas_call | solution.py:1326
  204.5 9.9 %shard_map.280 = (bf16[512,384]{1,0:T(8,128)(2,1)}, f32[512,384]{1,0:T(8,128)}, f32[768,1536]{1,0:T(8,128)}, f32[1536,768]{1,0:T(8,128)}, f32[1536,768]{1,0:T(8,...) custom-call(bf16[512,384]{1,0:T(8,128)(2,1)} %get-tuple-element.39.r, ...), custom_call_target="tpu_custom_call" | custom-call | tf_op jit(solution)/shard_map/pallas_call | solution.py:1360

commit v3 on v2

--- a/solution.py
+++ b/solution.py
@@ -955,20 +955,15 @@
         big_grad(r.part_select, r.select_low, r.normed[...], state)
         select_streams = [stream_start(bufs_select, 0)]
     stream_b(gate_streams[0])
-    stream_c(out_streams[2])
 
     if paired:
         pair_grad(r.part_value, r.gate, r.far_value, send_value, value_streams)
-        send_select.wait()
-        total = product(r.select_low[...], r.normed[:, own_half], 0, 0)
-        total = total + product(r.far_select[...], r.far_normed[...], 0, 0)
-        r.part_select[0] = total.astype(LOW)
-        stream_up(select_streams[0])
         for copy in send_hidden:
             copy.wait_send()
     else:
         for me in value_streams + select_streams:
             stream_a(me)
+    stream_c(out_streams[2])
     stream_b(gate_streams[1])
     stream_c(gate_streams[0])
 
@@ -1013,6 +1008,8 @@
     stream_b(value_streams[0])
     normed_last = spread_over(r.branch, r.normed_near, r.sent, r.normed_far, normed_copies)
     row_sums_end(r.mean_own, r.mean_held, mean_copies)
+    stream_c(gate_streams[2])
+    stream_b(value_streams[1])
     normed_last.wait()
 
     def input_rows(i, total):
@@ -1038,19 +1035,23 @@
     gain_grad = lax.fori_loop(0, total_rows // 32, input_rows, jnp.zeros((8, piece), WIDE))
     small[7:8, 0:piece] = jnp.sum(gain_grad, axis=0, keepdims=True)
 
+    if paired:
+        send_select.wait()
+        total = product(r.select_low[...], r.normed[:, own_half], 0, 0)
+        total = total + product(r.far_select[...], r.far_normed[...], 0, 0)
+        r.part_select[0] = total.astype(LOW)
+        stream_up(select_streams[0])
+
     small_copies = []
     for j in range(1, seq_count):
         copy = links.copy(small, r.small_seq.at[j - 1], {SEQ: lax.rem(s + j, seq_count)})
         copy.start()
         small_copies.append(copy)
-    stream_c(gate_streams[2])
-    stream_b(value_streams[1])
     stream_c(value_streams[0])
     stream_b(value_streams[2])
     stream_c(value_streams[1])
     stream_b(select_streams[0])
     stream_c(value_streams[2])
-    stream_c(select_streams[0])
     total = small[...]
     for j, copy in enumerate(small_copies):
         copy.wait()
@@ -1062,6 +1063,7 @@
         copy = links.copy(r.small_mid, r.small_dp.at[j - 1], {DP: lax.rem(d + j, dp_count)})
         copy.start()
         small_copies.append(copy)
+    stream_c(select_streams[0])
     for copy in small_copies:
         copy.wait()
     for j in range(dp_count - 1):

time: 216 us -> 211 us (0.977)
  Pallas kernels: 214 us -> 209 us
    pallas_call x1, Pallas kernels: 204 us -> 200 us  [body(): pl.pallas_call(functools.partial(mixer_kernel, facts), out_shape=[shape f...]
where the time goes in v3:
time: 211 us; the launch traced here: 210 us
  Pallas kernels  209 us (99%)
    pallas_call x1, Pallas kernels, body(): pl.pallas_call(functools.partial(mixer_kernel, facts), out_shape=[shape f...  200 us
    pallas_call x1, Pallas kernels, body(): pl.pallas_call(functools.partial(finish_kernel, half, heads, piece, inner...  9.89 us

profile of v3, /device:TPU:24, one launch (start us, length us, event | category | flops | bytes accessed | tf_op | source)
XLA Modules:
  0.0 210.3 jit_solution(5362517112381282577)
XLA Ops:
  0.7 199.6 %shard_map.279 = (bf16[512,384]{1,0:T(8,128)(2,1)}, f32[512,384]{1,0:T(8,128)}, f32[8,1024]{1,0:T(8,128)}, bf16[768,1536]{1,0:T(8,128)(2,1)}, bf16[1536,768]{1,0...) custom-call(bf16[512,384]{1,0:T(8,128)(2,1)} %bitcast.8, bf16[512,384]{1,0:T(8,128)(2,1)} %bitcast.9, ...), custom_call_target="tpu_custom_call" | custom-call | tf_op jit(solution)/shard_map/pallas_call | solution.py:1328
  200.2 9.9 %shard_map.280 = (bf16[512,384]{1,0:T(8,128)(2,1)}, f32[512,384]{1,0:T(8,128)}, f32[768,1536]{1,0:T(8,128)}, f32[1536,768]{1,0:T(8,128)}, f32[1536,768]{1,0:T(8,...) custom-call(bf16[512,384]{1,0:T(8,128)(2,1)} %get-tuple-element.39.r, ...), custom_call_target="tpu_custom_call" | custom-call | tf_op jit(solution)/shard_map/pallas_call | solution.py:1362
